TPU v7x, 32 devices: a whole 2x2x4 slice. The times are simulated.
32 devices in a mesh: gx: 8 (over y, x, core), gy: 4 (over z).
Axes of the slice: x: 2, y: 2, z: 4, core: 2. Of those that a mesh axis runs over, the one named last changes fastest.
Arguments:
- disc_pos: float32 [2, 32, 128, 128], P(None, 'gy', 'gx'), may hold values from 0 to 1
- disc_vel: float32 [2, 32, 128, 128], P(None, 'gy', 'gx'), may hold values from -3 to 3
- radius: float32 [32, 128, 128], P('gy', 'gx'), may hold values from 0.04 to 0.08
- bond_list: int32 [4, 32, 128, 128], P(None, 'gy', 'gx'), may hold values from 0 to 127
- contact_mask: int32 [8, 32, 128], P(None, 'gy', 'gx'), may hold values 0 or 1
- remap_block: int32 [32, 32, 8], P(('gx', 'gy')), may hold values from -1 to 127, as said below
- ocean_state: float32 [4, 48, 128, 1024], P(None, None, 'gy', 'gx'), may hold values from -6 to 6
- mix_coef: float32 [48, 128, 1024], P(None, 'gy', 'gx'), may hold values from 0.02 to 0.2
- remap_cell: int32 [32, 32, 8], P(('gx', 'gy')), may hold values from 0 to 4095
- fold_perm: int32 [1024], P('gx'), may hold values from 0 to 1023, as said below
Outputs:
- pos_next: float32 [2, 32, 128, 128], P(None, 'gy', 'gx')
- vel_next: float32 [2, 32, 128, 128], P(None, 'gy', 'gx')
- ocean_next: float32 [4, 48, 128, 1024], P(None, None, 'gy', 'gx')
Inputs may be any that keep to these rules, and one draw needn't show every extreme that they name: `remap_block`: for each ice tile, every one of its 128 local blocks stands in exactly one slot and the other slots hold -1; in every draw some ocean tile gets all 8 of its slots filled by every ice tile. `fold_perm`: A permutation of the 1024 columns.
All inputs are finite; a program needn't handle non-finite values. No bound on the sum of `contact_mask` on one device may be relied on, other than what follows from the above.
Results may differ from a plain program's by a relative error of at most 0.0003.
Values sent between devices are 32-bit elements; how exact they have to be, the bound alone decides.
No kernel may reach another device: no remote copies, remote signals or barrier semaphores. Data moves between devices by JAX's collectives and lax.ppermute only.
A program may use at most 128 MiB of HBM per device.

v0:
```python
import jax
import jax.numpy as jnp
from jax import lax
from jax.sharding import PartitionSpec as P

BONDS = 4
SUB = 3


SOFTEN = 0.0001
STIFFNESS = 2.0
BOND_STIFF = 0.1
TIME_STEP = 0.05
DRAG_ICE = 15.0
DRAG_BACK = 0.5
VERT_MIX = 0.1
SPIN_RATE = 0.3
ALL_SHIFTS = ((-1, -1), (-1, 0), (-1, 1), (0, -1), (0, 0), (0, 1), (1, -1), (1, 0), (1, 1))


def with_halo(block, sides, width, periodic):
    for axis, dim in sides:
        count = lax.axis_size(axis)
        forward = [(i, i + 1) for i in range(count - 1)]
        if periodic:
            forward.append((count - 1, 0))
        backward = [(target, source) for source, target in forward]
        low = lax.ppermute(
            lax.slice_in_dim(block, block.shape[dim] - width, None, axis=dim), axis, forward
        )
        high = lax.ppermute(lax.slice_in_dim(block, 0, width, axis=dim), axis, backward)
        block = jnp.concatenate([low, block, high], axis=dim)
    return block


def pair_force(own, other, shift_y, shift_x):
    sep_x = other[0][..., None, :] + shift_x - own[0][..., :, None]
    sep_y = other[1][..., None, :] + shift_y - own[1][..., :, None]
    distance = jnp.sqrt(sep_x * sep_x + sep_y * sep_y + SOFTEN)
    push = (
        STIFFNESS
        * jnp.maximum(own[2][..., :, None] + other[2][..., None, :] - distance, 0.0)
        / distance
    )
    return jnp.stack([-jnp.sum(push * sep_x, axis=-1), -jnp.sum(push * sep_y, axis=-1)])


def send_slots(values):
    return lax.all_to_all(values, ("gx", "gy"), split_axis=1, concat_axis=1, tiled=True)


def return_slots(values):
    return lax.all_to_all(values, ("gx", "gy"), split_axis=1, concat_axis=1, tiled=True)


def body(
    disc_pos,
    disc_vel,
    radius,
    bond_list,
    contact_mask,
    remap_block,
    ocean_state,
    mix_coef,
    remap_cell,
    fold_perm,
):
    rows_dev, cols_dev, disc_count = radius.shape
    block_count = rows_dev * cols_dev
    lat_tiles = lax.axis_size("gy")
    total_rows = rows_dev * lat_tiles
    global_rows = lax.axis_index("gy") * rows_dev + jnp.arange(rows_dev, dtype=jnp.int32)
    masked = contact_mask.astype(jnp.float32)
    weights = []
    counter = 0
    for shift_y, shift_x in ALL_SHIFTS:
        if shift_y == 0 and shift_x == 0:
            weights.append(jnp.ones((rows_dev, cols_dev), jnp.float32))
        else:
            inside = ((global_rows + shift_y >= 0) & (global_rows + shift_y < total_rows)).astype(
                jnp.float32
            )
            weights.append(masked[counter] * inside[:, None])
            counter = counter + 1
    mass = (radius / 0.06) ** 2
    disc_ids = jnp.arange(disc_count, dtype=jnp.int32)
    counts = jnp.zeros((rows_dev, cols_dev, disc_count, disc_count), jnp.float32)
    for partner in range(BONDS):
        counts = counts + (bond_list[partner][..., None] == disc_ids).astype(jnp.float32)
    position, velocity = (disc_pos, disc_vel)
    for substep in range(SUB):
        state = jnp.concatenate([position, radius[None]], axis=0)
        wide = with_halo(state, (("gx", 2),), 1, True)
        wide = with_halo(wide, (("gy", 1),), 1, False)
        contact = jnp.zeros((2, rows_dev, cols_dev, disc_count), jnp.float32)
        for index, (shift_y, shift_x) in enumerate(ALL_SHIFTS):
            other = wide[
                :, 1 + shift_y : 1 + shift_y + rows_dev, 1 + shift_x : 1 + shift_x + cols_dev
            ]
            contact = (
                contact
                + pair_force(state, other, float(shift_y), float(shift_x))
                * weights[index][None, :, :, None]
            )
        bonded = jnp.einsum("yxij,cyxj->cyxi", counts, position, precision=lax.Precision.HIGHEST)
        force = contact + BOND_STIFF * (bonded - BONDS * position)
        velocity = velocity + force / mass
        position = position + TIME_STEP * velocity
    impulse = (DRAG_ICE * jnp.sum(radius * radius * velocity, axis=-1)).reshape(2, block_count)
    source_count, tile_count, capacity = remap_block.shape
    selector = (
        remap_block[0].reshape(-1)[:, None] == jnp.arange(block_count, dtype=jnp.int32)[None]
    ).astype(jnp.float32)
    outgoing = jnp.dot(impulse, selector.T, precision=lax.Precision.HIGHEST).reshape(
        2, tile_count, capacity
    )
    arrived = send_slots(outgoing)
    layers, tile_rows, tile_cols = mix_coef.shape
    cells = remap_cell[0].reshape(-1)
    forcing = jax.ops.segment_sum(
        arrived.reshape(2, -1).T, cells, num_segments=tile_rows * tile_cols
    ).T
    forcing = forcing.reshape(2, tile_rows, tile_cols)
    lon_wide = with_halo(ocean_state, (("gx", 3),), 1, True)
    lat_wide = with_halo(ocean_state, (("gy", 2),), 1, False)
    top_row = ocean_state[:, :, tile_rows - 1]
    piece = lax.all_gather(top_row, "gx", axis=2, tiled=True)
    width = piece.shape[2]
    column_ids = jnp.arange(width, dtype=jnp.int32)
    picker = (column_ids[:, None] == fold_perm[None, :]).astype(jnp.float32)
    mirrored = jnp.einsum("fkw,wx->fkx", piece, picker, precision=lax.Precision.HIGHEST)
    signs = jnp.array([-1.0, -1.0, 1.0, 1.0], jnp.float32)[:, None, None]
    mirrored = signs * mirrored
    north = lat_wide[:, :, 2:]
    is_top = lax.axis_index("gy") == lat_tiles - 1
    last_row = jnp.where(is_top, mirrored, north[:, :, tile_rows - 1])
    north = jnp.concatenate([north[:, :, : tile_rows - 1], last_row[:, :, None]], axis=2)
    south = lat_wide[:, :, :tile_rows]
    east = lon_wide[..., 2:]
    west = lon_wide[..., :tile_cols]
    laplace = east + west + north + south - 4.0 * ocean_state
    above = jnp.concatenate([ocean_state[:, :1], ocean_state[:, :-1]], axis=1)
    below = jnp.concatenate([ocean_state[:, 1:], ocean_state[:, -1:]], axis=1)
    vertical = above + below - 2.0 * ocean_state
    updated = ocean_state + mix_coef[None] * laplace + VERT_MIX * vertical
    latitude = (lax.axis_index("gy") * tile_rows + jnp.arange(tile_rows, dtype=jnp.int32)).astype(
        jnp.float32
    )
    coriolis = (SPIN_RATE * (2.0 * (latitude + 0.5) / (tile_rows * lat_tiles) - 1.0))[None, :, None]
    updated = updated.at[0].add(coriolis * ocean_state[1])
    updated = updated.at[1].add(-coriolis * ocean_state[0])
    updated = updated.at[0:2, 0].add(forcing)
    surface = updated[0:2, 0].reshape(2, tile_rows * tile_cols)
    picked = jnp.take(surface, cells, axis=1).reshape(2, tile_count, capacity)
    returned = return_slots(picked)
    per_block = jnp.dot(returned.reshape(2, -1), selector, precision=lax.Precision.HIGHEST)
    per_block = per_block.reshape(2, rows_dev, cols_dev)
    vel_next = velocity + DRAG_BACK * (per_block[..., None] - velocity)
    return (position, vel_next, updated)


def solution(mesh):
    in_specs = (
        P(None, "gy", "gx", None),
        P(None, "gy", "gx", None),
        P("gy", "gx", None),
        P(None, "gy", "gx", None),
        P(None, "gy", "gx"),
        P(("gx", "gy"), None, None),
        P(None, None, "gy", "gx"),
        P(None, "gy", "gx"),
        P(("gx", "gy"), None, None),
        P("gx"),
    )
    out_specs = (P(None, "gy", "gx", None), P(None, "gy", "gx", None), P(None, None, "gy", "gx"))
    return jax.shard_map(body, mesh=mesh, in_specs=in_specs, out_specs=out_specs, check_vma=False)
```

profile of v0, /device:TPU:0, one launch (start us, length us, event | category | flops | bytes accessed | tf_op | source)
XLA Modules:
  0.0 526.0 jit_solution(14760382156335555216)
XLA Ops:
  3.0 3.4 collective-permute-start.1
  6.3 2.2 fusion.372
  8.5 4.1 collective-permute-start.15
  12.6 6.5 %fusion.373 = (f32[4,48,32,1]{3,2,1,0:T(8,128)}, f32[4,48,32,1]{3,2,1,0:T(8,128)}) fusion(f32[4,48,32,128]{3,2,1,0:T(8,128)} %param.23), kind=kLoop, calls=%fused_computation.611 | loop fusion | bytes 98304 | tf_op jit(solution)/shard_map/slice | solution.py:31
  19.1 3.7 copy.139
  22.9 3.6 copy.138
  26.5 2.6 collective-permute-start.12
  33.5 13.6 %all-gather = f32[4,48,1,1024]{3,1,0,2:T(8,128)} all-gather(f32[4,48,1,128]{3,1,0,2:T(8,128)} %bitcast.171), channel_id=2, replica_groups=mesh['gx'=8,'gy'=4] {'gx'}, dimensions={3}, use_global_device_ids=true | all-gather | bytes 884736 | tf_op jit(solution)/shard_map/all_gather | solution.py:127
  47.1 3.5 fusion.370
  59.3 2.2 slice.724
  65.6 5.2 collective-permute-start.2
  74.2 4.4 copy.114
  78.5 4.3 copy.116
  85.2 56.2 %fusion.3 = (f32[8,16,128]{2,1,0:T(8,128)S(1)}, f32[8,16,128]{2,1,0:T(8,128)S(1)}, f32[8,16,128]{2,1,0:T(8,128)S(1)}, f32[8,16,128]{2,1,0:T(8,128)S(1)}, f32[8,1...) fusion(f32[8,16,128]{2,1,0:T(8,128)S(1)} %copy-done.21, ...), kind=kLoop, calls=%fused_computation.116 | loop fusion | flops 188547072 | bytes 1966080 | tf_op jit(solution)/shard_map/reduce_sum | solution.py:45
  141.6 37.8 %fusion.12 = (f32[8,16,128]{2,1,0:T(8,128)S(1)}, f32[8,16,128]{2,1,0:T(8,128)S(1)}, f32[8,16,128]{2,1,0:T(8,128)S(1)}, f32[8,16,128]{2,1,0:T(8,128)S(1)}, f32[8,...) fusion(f32[8,16,128]{2,1,0:T(8,128)S(1)} %bitcast.299, f32[8,16,128]{2,1,0:T(8,128)S(1)} %copy-done.21, ...), kind=kLoop, calls=%fused_computation.125 | loop fusion | flops 94273536 | bytes 1179648 | tf_op jit(solution)/shard_map/reduce_sum | solution.py:45
  179.8 33.2 %multiply_add_fusion.3 = (f32[2,8,16,128]{3,0,2,1:T(2,128)S(1)}, f32[2,8,16,128]{3,0,2,1:T(2,128)S(1)}) fusion(f32[2,8,16,128]{3,2,1,0:T(8,128)S(1)} %copy-done.9, f32[8,16,128]{2,1,0:T(8,128)S(1)} %copy-done.12, s32[8,16,128]{2,1,0:T(8,128)S(1)} %copy-done.34, s32[8,16,128]{2,1,0:T(8,128)S(1)} %copy-done.36, s32[8,16,128]{2,1,0:T(8,128)S(1)} %copy-done.32, ...), kind=kOutput, calls=%fused_computation.518 | convolution fusion | flops 74481664 | bytes 2035712 | tf_op jit(solution)/shard_map/yxij,cyxj->cyxi/dot_general | solution.py:105
  213.1 2.6 collective-permute-start.5
  218.7 5.4 %collective-permute-start.6 = (f32[3,1,18,128]{3,0,2,1:T(4,128)S(1)}, f32[3,1,18,128]{3,0,2,1:T(4,128)S(1)}, u32[]{:S(2)}, u32[]{:S(2)}) collective-permute-start(f32[3,1,18,128]{3,0,2,1:T(4,128)S(1)} %get-tuple-element.213), channel_id=1, source_target_pairs={{0,1},{1,2},{2,3},{4,5},{5,6},{6,7},{8,9},{9,10},{10,11},{12,13},{... | collective-permute-start | bytes 82952 | tf_op jit(solution)/shard_map/ppermute | solution.py:28
  226.4 56.2 %fusion.83 = (f32[8,16,128]{2,1,0:T(8,128)S(1)}, f32[8,16,128]{2,1,0:T(8,128)S(1)}, f32[8,16,128]{2,1,0:T(8,128)S(1)}, f32[8,16,128]{2,1,0:T(8,128)S(1)}, f32[8,...) fusion(f32[8,16,128]{2,1,0:T(8,128)S(1)} %bitcast.400, ...), kind=kLoop, calls=%fused_computation.196 | loop fusion | flops 188547072 | bytes 1966080 | tf_op jit(solution)/shard_map/reduce_sum | solution.py:45
  282.6 37.8 %fusion.92 = (f32[8,16,128]{2,1,0:T(8,128)S(1)}, f32[8,16,128]{2,1,0:T(8,128)S(1)}, f32[8,16,128]{2,1,0:T(8,128)S(1)}, f32[8,16,128]{2,1,0:T(8,128)S(1)}, f32[8,...) fusion(f32[8,16,128]{2,1,0:T(8,128)S(1)} %bitcast.287, f32[8,16,128]{2,1,0:T(8,128)S(1)} %bitcast.401, ...), kind=kLoop, calls=%fused_computation.205 | loop fusion | flops 94273536 | bytes 1179648 | tf_op jit(solution)/shard_map/reduce_sum | solution.py:45
  320.7 27.2 %multiply_add_fusion.2 = (f32[2,8,16,128]{3,0,2,1:T(2,128)S(1)}, f32[2,8,16,128]{3,0,2,1:T(2,128)}) fusion(f32[2,8,16,128]{3,0,2,1:T(2,128)S(1)} %get-tuple-element.278, f32[2,8,16,128]{3,0,2,1:T(2,128)S(1)} %get-tuple-element.279, f32[8,16,128]{2,1,0:T(8,128)S(1)} %copy-done.12, s32[8,16,128]{2,1,0:T(8,128)S(1)} %copy-done.34, ...), kind=kOutput, calls=%fused_computation.517 | convolution fusion | flops 74481664 | bytes 2035712 | tf_op jit(solution)/shard_map/yxij,cyxj->cyxi/dot_general | solution.py:105
  348.1 2.6 collective-permute-start.9
  353.6 5.7 %collective-permute-start.10 = (f32[3,1,18,128]{3,0,2,1:T(4,128)S(1)}, f32[3,1,18,128]{3,0,2,1:T(4,128)}, u32[]{:S(2)}, u32[]{:S(2)}) collective-permute-start(f32[3,1,18,128]{3,0,2,1:T(4,128)S(1)} %get-tuple-element.211), channel_id=1, source_target_pairs={{0,1},{1,2},{2,3},{4,5},{5,6},{6,7},{8,9},{9,10},{10,11},{12,13},{... | collective-permute-start | bytes 82952 | tf_op jit(solution)/shard_map/ppermute | solution.py:28
  362.7 5.7 %fusion.259 = f32[4,48,32,128]{3,2,1,0:T(8,128)S(1)} fusion(f32[4,48,32,128]{3,2,1,0:T(8,128)S(1)} %copy-done, f32[4,48,1,128]{3,2,1,0:T(1,128)} %bitcast.155, f32[4,48,32,1]{3,2,1,0:T(8,128)S(1)} %copy-done.3, f32[4,48,32,1]{3,2,1,0:T(8,128)S(1)} %copy-done.2, f32[4,48,1,128]{3,2,1,0:T(1,128)S(1)} %bitcast.273, f32[4,48,31,128]{3,2,1,0:T(8,128)S(1)} %copy-done.1, ...), kind=kLoop, calls=%fused_computation.378 | loop fusion | flops 14155776 | bytes 16662528 | tf_op jit(solution)/shard_map/add | solution.py:145
  370.6 56.2 %fusion.163 = (f32[8,16,128]{2,1,0:T(8,128)S(1)}, f32[8,16,128]{2,1,0:T(8,128)S(1)}, f32[8,16,128]{2,1,0:T(8,128)S(1)}, f32[8,16,128]{2,1,0:T(8,128)S(1)}, f32[8...) fusion(f32[8,16,128]{2,1,0:T(8,128)S(1)} %bitcast.393, ...), kind=kLoop, calls=%fused_computation.276 | loop fusion | flops 188547072 | bytes 1966080 | tf_op jit(solution)/shard_map/reduce_sum | solution.py:45
  426.9 37.8 %fusion.172 = (f32[8,16,128]{2,1,0:T(8,128)S(1)}, f32[8,16,128]{2,1,0:T(8,128)S(1)}, f32[8,16,128]{2,1,0:T(8,128)S(1)}, f32[8,16,128]{2,1,0:T(8,128)S(1)}, f32[8...) fusion(f32[8,16,128]{2,1,0:T(8,128)S(1)} %bitcast.293, f32[8,16,128]{2,1,0:T(8,128)S(1)} %bitcast.394, ...), kind=kLoop, calls=%fused_computation.285 | loop fusion | flops 94273536 | bytes 1179648 | tf_op jit(solution)/shard_map/reduce_sum | solution.py:45
  465.1 28.4 %multiply_reduce_fusion = (f32[2,8,16]{0,2,1:T(8,128)S(1)}, f32[2,8,16,128]{3,0,2,1:T(2,128)S(1)}) fusion(f32[8,16,128]{2,1,0:T(8,128)S(1)} %copy-done.13, f32[2,8,16,128]{3,0,2,1:T(2,128)S(1)} %copy-done.57, f32[8,16,128]{2,1,0:T(8,128)S(1)} %copy-done.12, f32[2,8,16,128]{3,0,2,1:T(2,128)S(1)} %get-tuple-element.280, s32[8,16,128]{2,1,0:T(8,128)S(1)} %copy-done.35, ...), kind=kOutput, calls=%fused_computation.515 | convolution fusion | flops 74481408 | bytes 1971200 | tf_op jit(solution)/shard_map/yxij,cyxj->cyxi/dot_general | solution.py:105
  494.7 5.0 all-to-all-start
  499.7 2.2 fusion.285
  501.9 5.0 all-to-all-done
  513.7 2.6 all-to-all-start.1
  516.5 7.1 %all-to-all-done.1 = f32[2,32,8]{2,0,1:T(2,128)S(1)} async-done(((f32[2,32,8]{2,0,1:T(2,128)}), f32[2,32,8]{2,0,1:T(2,128)S(1)}, u32[]{:S(2)}, u32[]{:S(2)}) %all-to-all-start.1) | async-done | bytes 2080 | tf_op jit(solution)/shard_map/all_to_all | solution.py:53
  (263 shorter events, 49.3 us)
Async XLA Ops:
  3.0 59.9 %collective-permute-start.1 = (f32[3,8,1,128]{3,0,2,1:T(4,128)}, f32[3,8,1,128]{3,0,2,1:T(4,128)S(1)}, u32[]{:S(2)}, u32[]{:S(2)}) collective-permute-start(f32[3,8,1,128]{3,0,2,1:T(4,128)} %get-tuple-element.146), channel_id=1, source_target_pairs={{4,0},{8,4},{12,8},{16,12},{20,16},{24,20},{28,24},{0,28},{5,1},{9... | collective-permute-start | bytes 36872 | tf_op jit(solution)/shard_map/ppermute | solution.py:31
  6.3 56.5 %collective-permute-start = (f32[3,8,1,128]{3,0,2,1:T(4,128)}, f32[3,8,1,128]{3,0,2,1:T(4,128)}, u32[]{:S(2)}, u32[]{:S(2)}) collective-permute-start(f32[3,8,1,128]{3,0,2,1:T(4,128)} %get-tuple-element.264), channel_id=1, source_target_pairs={{0,4},{4,8},{8,12},{12,16},{16,20},{20,24},{24,28},{28,0},{1,5},{5... | collective-permute-start | bytes 36872 | tf_op jit(solution)/shard_map/ppermute | solution.py:28
  8.5 354.1 %collective-permute-start.15 = (f32[4,48,1,128]{3,1,0,2:T(8,128)}, f32[4,48,1,128]{3,1,0,2:T(8,128)}, u32[]{:S(2)}, u32[]{:S(2)}) collective-permute-start(f32[4,48,1,128]{3,1,0,2:T(8,128)} %bitcast.171), channel_id=1, source_target_pairs={{0,1},{1,2},{2,3},{4,5},{5,6},{6,7},{8,9},{9,10},{10,11},{12,13},{... | collective-permute-start | bytes 294920 | tf_op jit(solution)/shard_map/ppermute | solution.py:28
  22.9 55.6 %collective-permute-start.13 = (f32[4,48,32,1]{1,2,3,0:T(8,128)}, f32[4,48,32,1]{1,2,3,0:T(8,128)}, u32[]{:S(2)}, u32[]{:S(2)}) collective-permute-start(f32[4,48,32,1]{1,2,3,0:T(8,128)} %copy.139), channel_id=1, source_target_pairs={{0,4},{4,8},{8,12},{12,16},{16,20},{20,24},{24,28},{28,0},{1,5},{5... | collective-permute-start | bytes 73736 | tf_op jit(solution)/shard_map/ppermute | solution.py:28
  26.5 46.2 %collective-permute-start.12 = (f32[4,48,32,1]{1,2,3,0:T(8,128)}, f32[4,48,32,1]{1,2,3,0:T(8,128)}, u32[]{:S(2)}, u32[]{:S(2)}) collective-permute-start(f32[4,48,32,1]{1,2,3,0:T(8,128)} %copy.138), channel_id=1, source_target_pairs={{4,0},{8,4},{12,8},{16,12},{20,16},{24,20},{28,24},{0,28},{5,1},{9... | collective-permute-start | bytes 73736 | tf_op jit(solution)/shard_map/ppermute | solution.py:31
  64.3 18.6 %collective-permute-start.3 = (f32[3,1,18,128]{3,0,2,1:T(4,128)}, f32[3,1,18,128]{3,0,2,1:T(4,128)}, u32[]{:S(2)}, u32[]{:S(2)}) collective-permute-start(f32[3,1,18,128]{3,0,2,1:T(4,128)} %get-tuple-element.214), channel_id=1, source_target_pairs={{1,0},{2,1},{3,2},{5,4},{6,5},{7,6},{9,8},{10,9},{11,10},{13,12},{... | collective-permute-start | bytes 82952 | tf_op jit(solution)/shard_map/ppermute | solution.py:31
  65.6 17.3 %collective-permute-start.2 = (f32[3,1,18,128]{3,0,2,1:T(4,128)}, f32[3,1,18,128]{3,0,2,1:T(4,128)}, u32[]{:S(2)}, u32[]{:S(2)}) collective-permute-start(f32[3,1,18,128]{3,0,2,1:T(4,128)} %get-tuple-element.215), channel_id=1, source_target_pairs={{0,1},{1,2},{2,3},{4,5},{5,6},{6,7},{8,9},{9,10},{10,11},{12,13},{... | collective-permute-start | bytes 82952 | tf_op jit(solution)/shard_map/ppermute | solution.py:28
  72.7 288.4 %collective-permute-start.14 = (f32[4,48,1,128]{3,1,0,2:T(8,128)}, f32[4,48,1,128]{3,1,0,2:T(8,128)}, u32[]{:S(2)}, u32[]{:S(2)}) collective-permute-start(f32[4,48,1,128]{3,1,0,2:T(8,128)} %bitcast.276), channel_id=1, source_target_pairs={{1,0},{2,1},{3,2},{5,4},{6,5},{7,6},{9,8},{10,9},{11,10},{13,12},{... | collective-permute-start | bytes 294920 | tf_op jit(solution)/shard_map/ppermute | solution.py:31
  85.2 56.2 %copy-start.14 = (f32[1,8,16,128]{3,0,2,1:T(1,128)S(1)}, f32[1,8,16,128]{3,0,2,1:T(1,128)}, u32[]{:S(2)}) copy-start(f32[1,8,16,128]{3,0,2,1:T(1,128)} %get-tuple-element.228) | copy-start | bytes 196612
  85.2 56.2 %copy-start.15 = (f32[1,8,16,128]{3,0,2,1:T(1,128)S(1)}, f32[1,8,16,128]{3,0,2,1:T(1,128)}, u32[]{:S(2)}) copy-start(f32[1,8,16,128]{3,0,2,1:T(1,128)} %get-tuple-element.229) | copy-start | bytes 196612
  85.2 56.2 %copy-start.16 = (f32[1,8,16,128]{3,0,2,1:T(1,128)S(1)}, f32[1,8,16,128]{3,0,2,1:T(1,128)}, u32[]{:S(2)}) copy-start(f32[1,8,16,128]{3,0,2,1:T(1,128)} %get-tuple-element.230) | copy-start | bytes 196612
  213.1 4.1 collective-permute-start.4
  213.1 4.1 collective-permute-start.5
  217.4 7.2 %collective-permute-start.7 = (f32[3,1,18,128]{3,0,2,1:T(4,128)S(1)}, f32[3,1,18,128]{3,0,2,1:T(4,128)S(1)}, u32[]{:S(2)}, u32[]{:S(2)}) collective-permute-start(f32[3,1,18,128]{3,0,2,1:T(4,128)S(1)} %get-tuple-element.212), channel_id=1, source_target_pairs={{1,0},{2,1},{3,2},{5,4},{6,5},{7,6},{9,8},{10,9},{11,10},{13,12},{... | collective-permute-start | bytes 82952 | tf_op jit(solution)/shard_map/ppermute | solution.py:31
  218.7 6.8 %collective-permute-start.6 = (f32[3,1,18,128]{3,0,2,1:T(4,128)S(1)}, f32[3,1,18,128]{3,0,2,1:T(4,128)S(1)}, u32[]{:S(2)}, u32[]{:S(2)}) collective-permute-start(f32[3,1,18,128]{3,0,2,1:T(4,128)S(1)} %get-tuple-element.213), channel_id=1, source_target_pairs={{0,1},{1,2},{2,3},{4,5},{5,6},{6,7},{8,9},{9,10},{10,11},{12,13},{... | collective-permute-start | bytes 82952 | tf_op jit(solution)/shard_map/ppermute | solution.py:28
  320.7 40.4 %copy-start.8 = (f32[4,48,1,1024]{3,1,0,2:T(8,128)S(1)}, f32[4,48,1,1024]{3,1,0,2:T(8,128)}, u32[]{:S(2)}) copy-start(f32[4,48,1,1024]{3,1,0,2:T(8,128)} %all-gather) | copy-start | bytes 2359300
  320.7 40.4 %copy-start.52 = (s32[128]{0:T(128)S(1)}, s32[128]{0:T(128)}, u32[]{:S(2)}) copy-start(s32[128]{0:T(128)} %param.26) | copy-start | bytes 1540
  320.7 40.4 %copy-start.54 = (f32[4]{0:T(128)S(1)}, f32[4]{0:T(128)}, u32[]{:S(2)}) copy-start(f32[4]{0:T(128)} %constant.157.clone) | copy-start | bytes 52
  320.7 41.9 %copy-start.2 = (f32[4,48,32,1]{3,2,1,0:T(8,128)S(1)}, f32[4,48,32,1]{3,2,1,0:T(8,128)}, u32[]{:S(2)}) copy-start(f32[4,48,32,1]{3,2,1,0:T(8,128)} %copy.114) | copy-start | bytes 73732
  320.7 41.9 %copy-start.3 = (f32[4,48,32,1]{3,2,1,0:T(8,128)S(1)}, f32[4,48,32,1]{3,2,1,0:T(8,128)}, u32[]{:S(2)}) copy-start(f32[4,48,32,1]{3,2,1,0:T(8,128)} %copy.116) | copy-start | bytes 73732
  320.7 41.9 %copy-start.4 = (f32[4,47,32,128]{3,2,1,0:T(8,128)S(1)}, f32[4,47,32,128]{3,2,1,0:T(8,128)}, u32[]{:S(2)}) copy-start(f32[4,47,32,128]{3,2,1,0:T(8,128)} %get-tuple-element.148) | copy-start | bytes 9240580
  320.7 41.9 %copy-start.5 = (f32[4,47,32,128]{3,2,1,0:T(8,128)S(1)}, f32[4,47,32,128]{3,2,1,0:T(8,128)}, u32[]{:S(2)}) copy-start(f32[4,47,32,128]{3,2,1,0:T(8,128)} %get-tuple-element.149) | copy-start | bytes 9240580
  348.0 4.1 collective-permute-start.8
  348.1 4.1 collective-permute-start.9
  352.3 16.4 %collective-permute-start.11 = (f32[3,1,18,128]{3,0,2,1:T(4,128)S(1)}, f32[3,1,18,128]{3,0,2,1:T(4,128)S(1)}, u32[]{:S(2)}, u32[]{:S(2)}) collective-permute-start(f32[3,1,18,128]{3,0,2,1:T(4,128)S(1)} %get-tuple-element.210), channel_id=1, source_target_pairs={{1,0},{2,1},{3,2},{5,4},{6,5},{7,6},{9,8},{10,9},{11,10},{13,12},{... | collective-permute-start | bytes 82952 | tf_op jit(solution)/shard_map/ppermute | solution.py:31
  353.6 15.1 %collective-permute-start.10 = (f32[3,1,18,128]{3,0,2,1:T(4,128)S(1)}, f32[3,1,18,128]{3,0,2,1:T(4,128)}, u32[]{:S(2)}, u32[]{:S(2)}) collective-permute-start(f32[3,1,18,128]{3,0,2,1:T(4,128)S(1)} %get-tuple-element.211), channel_id=1, source_target_pairs={{0,1},{1,2},{2,3},{4,5},{5,6},{6,7},{8,9},{9,10},{10,11},{12,13},{... | collective-permute-start | bytes 82952 | tf_op jit(solution)/shard_map/ppermute | solution.py:28
  368.7 58.0 %copy-start.7 = (f32[4,48,32,128]{3,2,1,0:T(8,128)}, f32[4,48,32,128]{3,2,1,0:T(8,128)S(1)}, u32[]{:S(2)}) copy-start(f32[4,48,32,128]{3,2,1,0:T(8,128)S(1)} %fusion.286) | copy-start | bytes 9437188
  370.5 56.2 %copy-start.24 = (f32[1,8,16,128]{3,0,2,1:T(1,128)S(1)}, f32[1,8,16,128]{3,0,2,1:T(1,128)}, u32[]{:S(2)}) copy-start(f32[1,8,16,128]{3,0,2,1:T(1,128)} %get-tuple-element.216) | copy-start | bytes 196612
  370.6 56.2 %copy-start.25 = (f32[1,8,16,128]{3,0,2,1:T(1,128)S(1)}, f32[1,8,16,128]{3,0,2,1:T(1,128)}, u32[]{:S(2)}) copy-start(f32[1,8,16,128]{3,0,2,1:T(1,128)} %get-tuple-element.217) | copy-start | bytes 196612
  370.6 56.2 %copy-start.26 = (f32[1,8,16,128]{3,0,2,1:T(1,128)S(1)}, f32[1,8,16,128]{3,0,2,1:T(1,128)}, u32[]{:S(2)}) copy-start(f32[1,8,16,128]{3,0,2,1:T(1,128)} %get-tuple-element.218) | copy-start | bytes 196612
  494.7 12.3 %all-to-all-start = ((f32[2,32,8]{2,0,1:T(2,128)}), f32[2,32,8]{2,0,1:T(2,128)S(1)}, u32[]{:S(2)}, u32[]{:S(2)}) async-start(f32[2,32,8]{2,0,1:T(2,128)} %copy.123), calls=%async_computation | async-start | bytes 65536 | tf_op jit(solution)/shard_map/all_to_all | solution.py:49
  513.7 9.9 %all-to-all-start.1 = ((f32[2,32,8]{2,0,1:T(2,128)}), f32[2,32,8]{2,0,1:T(2,128)S(1)}, u32[]{:S(2)}, u32[]{:S(2)}) async-start(f32[2,32,8]{2,0,1:T(2,128)} %broadcast_select_fusion), calls=%async_computation.1 | async-start | bytes 65536 | tf_op jit(solution)/shard_map/all_to_all | solution.py:53
  (44 other events, 1088.0 us)
where the time goes:
time: 532 us; the launch traced here: 526 us
  other arithmetic  313 us (59%)
  matrix products  91 us (17%)
  local copies, waits for them, and re-layouts  45.7 us (9%)
  starting transfers between devices  44.7 us (8%)
  waiting for transfers between devices  15.2 us (3%)
  blocking collectives  13.6 us (3%)
    reduce_sum x6, other arithmetic, pair_force(): jnp.sum(push * sep_x, axis=-1)  282 us
    dot_general x3, matrix products, body(): jnp.einsum('yxij,cyxj->cyxi', counts, position, precision=lax.Precision.H...  88.8 us
    ppermute x8, starting transfers between devices, with_halo(): lax.ppermute(lax.slice_in_dim(block, block.shape[dim] - width, None, axis...  20.5 us
    ppermute x8, starting transfers between devices, with_halo(): lax.ppermute(lax.slice_in_dim(block, 0, width, axis=dim), axis, backward)  16.6 us
    all_gather x1, blocking collectives, body(): piece = lax.all_gather(top_row, 'gx', axis=2, tiled=True)  13.6 us
    unnamed x123, local copies, waits for them, and re-layouts  10.7 us
  transfers between devices with their start and end apart: 18, of which 5 were waited for; matrix products, arithmetic and copies ran while one was open for 60% of the time, Pallas kernels for 0%

commit v1 on v0

v1 whole, which is shorter than its diff:
```python
import functools

import jax
import jax.numpy as jnp
import numpy as np
from jax import lax
from jax.experimental import pallas as pl
from jax.experimental.pallas import tpu as pltpu
from jax.sharding import PartitionSpec as P

BONDS = 4
SUB = 3


SOFTEN = 0.0001
STIFFNESS = 2.0
BOND_STIFF = 0.1
TIME_STEP = 0.05
DRAG_ICE = 15.0
DRAG_BACK = 0.5
VERT_MIX = 0.1
SPIN_RATE = 0.3
ALL_SHIFTS = ((-1, -1), (-1, 0), (-1, 1), (0, -1), (0, 0), (0, 1), (1, -1), (1, 0), (1, 1))
CENTER = 4
UNROLL = 16
DEPTH = 80
HIGHEST = lax.Precision.HIGHEST


def shift_tables():
    add = np.zeros((9, 32, 384), np.float32)
    scale = np.zeros((9, 32, 128), np.float32)
    for s, (sy, sx) in enumerate(ALL_SHIFTS):
        for g in (0, 8, 16):
            add[s, g, :128] = 2 * sx
            add[s, g + 1, :128] = 2 * sy
        add[s, 3, :128] = sx * sx + sy * sy
        add[s, 30, 128:256] = sx
        add[s, 30, 256:] = sy
        scale[s, 24:27] = -2 * sx
        scale[s, 27:30] = -2 * sy
    return add, scale


def pair_codes(rows, cols):
    own = rows * cols
    base_left, base_right = own, own + rows
    base_low = own + 2 * rows
    base_high = base_low + cols + 2
    code = np.zeros((own, 9), np.int32)
    for y in range(rows):
        for x in range(cols):
            for s, (sy, sx) in enumerate(ALL_SHIFTS):
                ny, nx = y + sy, x + sx
                if ny < 0:
                    j = base_low + nx + 1
                elif ny >= rows:
                    j = base_high + nx + 1
                elif nx < 0:
                    j = base_left + ny
                elif nx >= cols:
                    j = base_right + ny
                else:
                    j = ny * cols + nx
                code[y * cols + x, s] = ((y * cols + x) * 256 + j) * 16 + s
    return code.reshape(-1), base_high + cols + 2


def list_kernel(active_ref, code_ref, inner_ref, outer_ref, count_ref, *, own):
    def step(i, counts):
        inner, outer = counts
        others = 0
        for s in range(9):
            code = code_ref[i * 9 + s]
            inner_ref[inner] = code
            if s == CENTER:
                inner = inner + 1
                continue
            outer_ref[outer] = code
            flag = active_ref[others * own + i]
            away = (((code >> 4) & 255) >= own).astype(jnp.int32) * flag
            inner = inner + (flag - away)
            outer = outer + away
            others = others + 1
        return inner, outer

    inner, outer = lax.fori_loop(0, own, step, (jnp.int32(0), jnp.int32(0)))
    for u in range(UNROLL):
        inner_ref[inner + u] = jnp.int32((own * 256) * 16 + CENTER)
        outer_ref[outer + u] = jnp.int32((own * 256 + own) * 16 + CENTER)
    count_ref[0] = inner
    count_ref[1] = outer


def top_bits(value):
    scaled = value * 65537.0
    return scaled - (scaled - value)


def split(tile):
    high = top_bits(tile)
    rest = tile - high
    mid = top_bits(rest)
    return high, mid, rest - mid


def far_features(tile, at_ref, index):
    high, mid, low = split(tile)
    stack = [high, high, mid, mid, high, low, high, mid, low, jnp.ones((8, 128), jnp.float32)]
    at_ref[index] = jnp.concatenate(stack, axis=0).T.astype(jnp.bfloat16)
    return high, mid, low


def near_features(parts, head_ref, tail_ref, index):
    row_id = lax.broadcasted_iota(jnp.int32, (8, 128), 0)
    zero8 = jnp.zeros((8, 128), jnp.float32)
    dist_scale = jnp.where(row_id < 2, -2.0, jnp.where(row_id < 4, 1.0, 0.0))
    reach_scale = jnp.where((row_id == 4) | (row_id == 5), 1.0, 0.0)
    swap_up = (row_id == 3) | (row_id == 5)
    swap_down = (row_id == 2) | (row_id == 4)
    only_x = jnp.where(row_id == 0, 1.0, 0.0)
    only_y = jnp.where(row_id == 1, 1.0, 0.0)

    def swapped(tile):
        up = pltpu.roll(tile, 1, 0)
        down = pltpu.roll(tile, 7, 0)
        return jnp.where(swap_up, up, jnp.where(swap_down, down, tile))

    def gathered(row):
        rows = [jnp.broadcast_to(part[row : row + 1], (8, 128)) for part in parts]
        picked = jnp.where(row_id == 0, rows[0], jnp.where(row_id == 1, rows[1], rows[2]))
        return jnp.where(row_id < 3, picked, 0.0)

    high, mid, low = [swapped(part) for part in parts]
    order = [high, mid, high, mid, low, high]
    dist = jnp.concatenate([part * dist_scale for part in order], axis=0)
    reach = jnp.concatenate([part * reach_scale for part in order], axis=0)
    off_x = jnp.concatenate([only_x, zero8, only_x, zero8, zero8, only_x], axis=0)
    off_y = jnp.concatenate([only_y, zero8, only_y, zero8, zero8, only_y], axis=0)
    head_ref[index] = jnp.concatenate([dist, off_x, off_y, reach], axis=1).astype(jnp.bfloat16)
    first = gathered(0)
    second = gathered(1)
    both = first + pltpu.roll(second, 3, 0)
    zero24 = jnp.zeros((24, 384), jnp.float32)
    last = jnp.concatenate([both, -first, -second], axis=1)
    tail_ref[index] = jnp.concatenate([zero24, last], axis=0).astype(jnp.bfloat16)


def clear_spare(own, head_ref, tail_ref, acc_ref):
    head_ref[own] = jnp.zeros((48, 512), jnp.bfloat16)
    tail_ref[own] = jnp.zeros((32, 384), jnp.bfloat16)
    acc_ref[own] = jnp.zeros((16, 128), jnp.float32)


def visit(count, list_ref, far_base, at_ref, head_ref, tail_ref, add_ref, scale_ref, acc_ref):
    pad = jnp.zeros((32, 128), jnp.bfloat16)

    def pairs(step, carry):
        for u in range(UNROLL):
            code = list_ref[step * UNROLL + u]
            s = code & 15
            j = ((code >> 4) & 255) - far_base
            i = code >> 12
            tail = tail_ref[i]
            dist = tail[:, :128] * scale_ref[s]
            tail = jnp.concatenate([dist, tail[:, 128:]], axis=1) + add_ref[s]
            near = jnp.concatenate(
                [head_ref[i], jnp.concatenate([tail, pad], axis=1)], axis=0
            )
            every = jnp.dot(at_ref[j], near, preferred_element_type=jnp.float32)
            square = jnp.maximum(every[:, :128], SOFTEN)
            push = jnp.maximum(every[:, 384:] * lax.rsqrt(square) - 1.0, 0.0)
            sum_x = jnp.sum((push * every[:, 128:256]).reshape(16, 8, 128), axis=0)
            sum_y = jnp.sum((push * every[:, 256:384]).reshape(16, 8, 128), axis=0)
            acc_ref[i] = acc_ref[i] + jnp.concatenate([sum_x, sum_y], axis=0)
        return carry

    lax.fori_loop(0, (count + (UNROLL - 1)) // UNROLL, pairs, 0)


def inner_kernel(
    count_ref, list_ref, own_ref, add_ref, scale_ref, acc_ref, at_ref, head_ref, tail_ref
):
    own = own_ref.shape[0]

    def build(b, carry):
        parts = far_features(own_ref[b], at_ref, b)
        near_features(parts, head_ref, tail_ref, b)
        acc_ref[b] = jnp.zeros((16, 128), jnp.float32)
        return carry

    lax.fori_loop(0, own, build, 0, unroll=4)
    clear_spare(own, head_ref, tail_ref, acc_ref)
    visit(
        count_ref[0], list_ref, 0, at_ref, head_ref, tail_ref, add_ref, scale_ref, acc_ref
    )


def outer_kernel(
    count_ref,
    list_ref,
    own_ref,
    left_ref,
    right_ref,
    low_ref,
    high_ref,
    vel_ref,
    bond_ref,
    add_ref,
    scale_ref,
    inner_ref,
    next_ref,
    velnext_ref,
    at_ref,
    head_ref,
    tail_ref,
    acc_ref,
):
    own = own_ref.shape[0]
    rows = left_ref.shape[0]
    cols = own // rows

    def build(b):
        near_features(split(own_ref[b]), head_ref, tail_ref, b)

    def build_column(y, carry):
        build(y * cols)
        build(y * cols + cols - 1)
        return carry

    def build_row(x, carry):
        build(x)
        build((rows - 1) * cols + x)
        return carry

    lax.fori_loop(0, rows, build_column, 0, unroll=2)
    lax.fori_loop(1, cols - 1, build_row, 0, unroll=2)

    def clear(b, carry):
        acc_ref[b] = jnp.zeros((16, 128), jnp.float32)
        return carry

    lax.fori_loop(0, own, clear, 0, unroll=8)
    clear_spare(own, head_ref, tail_ref, acc_ref)
    base = 0
    for ref in (left_ref, right_ref, low_ref, high_ref):

        def build_halo(b, carry, ref=ref, base=base):
            far_features(ref[b], at_ref, base + b)
            return carry

        lax.fori_loop(0, ref.shape[0], build_halo, 0, unroll=2)
        base = base + ref.shape[0]
    visit(
        count_ref[1], list_ref, own, at_ref, head_ref, tail_ref, add_ref, scale_ref, acc_ref
    )
    row_id = lax.broadcasted_iota(jnp.int32, (8, 128), 0)

    def update(b, carry):
        tile = own_ref[b]
        vel = vel_ref[b]
        acc = acc_ref[b] + inner_ref[b]
        sum_x = jnp.sum(acc[:8], axis=0, keepdims=True)
        sum_y = jnp.sum(acc[8:], axis=0, keepdims=True)
        contact = -STIFFNESS * jnp.where(row_id == 0, sum_x, sum_y)
        bonded = -float(BONDS) * tile
        for partner in range(BONDS):
            index = jnp.broadcast_to(bond_ref[partner, pl.ds(b, 1), :], (8, 128))
            bonded = bonded + jnp.take_along_axis(
                tile, index, axis=1, mode="promise_in_bounds"
            )
        force = contact + BOND_STIFF * bonded
        over_mass = jnp.broadcast_to(vel[2:3], (8, 128))
        new_vel = vel + force * over_mass
        new_pos = tile + TIME_STEP * new_vel
        square = new_pos * new_pos
        length = pltpu.roll(square, 2, 0) + pltpu.roll(square, 1, 0) + 0.5 * SOFTEN
        next_ref[b] = jnp.where(row_id < 2, new_pos, jnp.where(row_id == 2, length, tile))
        velnext_ref[b] = jnp.where(row_id < 2, new_vel, vel)
        return carry

    lax.fori_loop(0, own, update, 0, unroll=4)


def smem():
    return pl.BlockSpec(memory_space=pltpu.MemorySpace.SMEM)


def vmem():
    return pl.BlockSpec(memory_space=pltpu.MemorySpace.VMEM)


def edge_kernel(ocean_ref, edge_ref, south_ref, north_ref, *, rows):
    total, lanes = ocean_ref.shape
    count = total // lanes
    lane = lax.broadcasted_iota(jnp.int32, (lanes, lanes), 1)
    wide = jnp.zeros((lanes, lanes), jnp.float32)
    for q in range(count):
        part = ocean_ref[q * lanes : (q + 1) * lanes, :]
        wide = jnp.where(lane == q, pltpu.roll(part, (q + 1) % lanes, 1), wide)
        wide = jnp.where(lane == lanes // 2 + q, pltpu.roll(part, lanes // 2 + q, 1), wide)
    edge_ref[...] = wide.T
    south_ref[...] = ocean_ref[pl.ds(0, total // rows, rows), :]
    north_ref[...] = ocean_ref[pl.ds(rows - 1, total // rows, rows), :]


def ocean_kernel(
    flags_ref,
    ocean_ref,
    before_ref,
    after_ref,
    mix_ref,
    west_ref,
    east_ref,
    south_ref,
    north_ref,
    top_ref,
    perm_ref,
    cor_ref,
    out_ref,
    fold_ref,
    wcol_ref,
    ecol_ref,
):
    fields, chunk, rows, lanes = ocean_ref.shape
    layers = south_ref.shape[0] // fields
    planes = fields * layers

    @pl.when(pl.program_id(0) == 0)
    def _():
        columns = jnp.broadcast_to(perm_ref[...], (planes, lanes))
        mirrored = jnp.zeros((planes, lanes), jnp.float32)
        for source in range(top_ref.shape[0]):
            picked = jnp.take_along_axis(
                top_ref[source], columns & (lanes - 1), axis=1, mode="promise_in_bounds"
            )
            mirrored = jnp.where(columns // lanes == source, picked, mirrored)
        plane_id = lax.broadcasted_iota(jnp.int32, (planes, lanes), 0)
        mirrored = jnp.where(plane_id < 2 * layers, -mirrored, mirrored)
        fold_ref[...] = jnp.where(flags_ref[0] > 0, mirrored, north_ref[...])
        pad = jnp.zeros((lanes - west_ref.shape[0], lanes), jnp.float32)
        wcol_ref[...] = jnp.concatenate([west_ref[...], pad], axis=0).T
        ecol_ref[...] = jnp.concatenate([east_ref[...], pad], axis=0).T

    per = lanes // rows
    lane = lax.broadcasted_iota(jnp.int32, (rows, lanes), 1)
    row = lax.broadcasted_iota(jnp.int32, (rows, lanes), 0)
    cor = cor_ref[...]
    for local in range(chunk):
        k = pl.program_id(0) * chunk + local
        mix = mix_ref[local]
        old = [ocean_ref[f, local] for f in range(fields)]
        for f in range(fields):
            here = old[f]
            plane = f * layers + k
            place = jnp.full((rows, lanes), plane // per, jnp.int32)
            start = pl.multiple_of((plane % per) * rows, 8)
            wcol = jnp.take_along_axis(
                wcol_ref[pl.ds(start, rows), :], place, axis=1, mode="promise_in_bounds"
            )
            ecol = jnp.take_along_axis(
                ecol_ref[pl.ds(start, rows), :], place, axis=1, mode="promise_in_bounds"
            )
            west = jnp.where(lane == 0, wcol, pltpu.roll(here, 1, 1))
            east = jnp.where(lane == lanes - 1, ecol, pltpu.roll(here, lanes - 1, 1))
            below_row = jnp.broadcast_to(south_ref[pl.ds(plane, 1), :], (rows, lanes))
            above_row = jnp.broadcast_to(fold_ref[pl.ds(plane, 1), :], (rows, lanes))
            south = jnp.where(row == 0, below_row, pltpu.roll(here, 1, 0))
            north = jnp.where(row == rows - 1, above_row, pltpu.roll(here, rows - 1, 0))
            laplace = east + west + north + south - 4.0 * here
            above = before_ref[f, 0] if local == 0 else ocean_ref[f, local - 1]
            below = after_ref[f, 0] if local == chunk - 1 else ocean_ref[f, local + 1]
            vertical = above + below - 2.0 * here
            new = here + mix * laplace + VERT_MIX * vertical
            if f == 0:
                new = new + cor * old[1]
            elif f == 1:
                new = new - cor * old[0]
            out_ref[f, local] = new


def ring(axis, step):
    count = lax.axis_size(axis)
    return [(i, (i + step) % count) for i in range(count)]


def line(axis, step):
    count = lax.axis_size(axis)
    return [(i, i + step) for i in range(count) if 0 <= i + step < count]


def halos(state):
    rows, cols = state.shape[:2]
    left = lax.ppermute(state[:, cols - 1], "gx", ring("gx", 1))
    right = lax.ppermute(state[:, 0], "gx", ring("gx", -1))
    bottom = jnp.concatenate([left[:1], state[0], right[:1]], axis=0)
    top = jnp.concatenate([left[rows - 1 :], state[rows - 1], right[rows - 1 :]], axis=0)
    state, bottom, top = lax.optimization_barrier((state, bottom, top))
    low = lax.ppermute(top, "gy", line("gy", 1))
    high = lax.ppermute(bottom, "gy", line("gy", -1))
    return state, left, right, low, high


def body(
    disc_pos,
    disc_vel,
    radius,
    bond_list,
    contact_mask,
    remap_block,
    ocean_state,
    mix_coef,
    remap_cell,
    fold_perm,
):
    rows_dev, cols_dev, disc_count = radius.shape
    block_count = rows_dev * cols_dev
    lat_tiles = lax.axis_size("gy")
    total_rows = rows_dev * lat_tiles
    _, tile_count, capacity = remap_block.shape
    slots = tile_count * capacity
    fields, layers, tile_rows, tile_cols = ocean_state.shape
    planes = fields * layers
    f32 = jnp.float32

    edge_rows = tile_cols // 2
    edges, south_row, north_row = pl.pallas_call(
        functools.partial(edge_kernel, rows=tile_rows),
        out_shape=(
            jax.ShapeDtypeStruct((tile_cols, tile_cols), f32),
            jax.ShapeDtypeStruct((planes, tile_cols), f32),
            jax.ShapeDtypeStruct((planes, tile_cols), f32),
        ),
        cost_estimate=pl.CostEstimate(flops=10**7, transcendentals=0, bytes_accessed=4 * 10**6),
        name="edges",
    )(ocean_state.reshape(planes * tile_rows, tile_cols))
    west = lax.ppermute(edges[:edge_rows], "gx", ring("gx", 1))
    east = lax.ppermute(edges[edge_rows:], "gx", ring("gx", -1))
    from_south = lax.ppermute(north_row, "gy", line("gy", 1))
    from_north = lax.ppermute(south_row, "gy", line("gy", -1))
    lon_tiles = lax.axis_size("gx")
    tops = lax.all_to_all(
        jnp.broadcast_to(north_row[None], (lon_tiles, planes, tile_cols)),
        "gx",
        split_axis=0,
        concat_axis=0,
        tiled=True,
    )

    global_rows = lax.axis_index("gy") * rows_dev + jnp.arange(rows_dev, dtype=jnp.int32)
    shift_rows = jnp.asarray([sy for sy, sx in ALL_SHIFTS if (sy, sx) != (0, 0)], jnp.int32)
    other_rows = shift_rows[:, None] + global_rows[None]
    inside = (other_rows >= 0) & (other_rows < total_rows)
    active = jnp.where(inside[:, :, None], contact_mask, 0).reshape(-1)
    codes, wide_count = pair_codes(rows_dev, cols_dev)
    list_shape = jax.ShapeDtypeStruct((block_count * 9 + UNROLL,), jnp.int32)
    inner_list, outer_list, pair_count = pl.pallas_call(
        functools.partial(list_kernel, own=block_count),
        in_specs=[smem(), smem()],
        out_specs=(smem(), smem(), smem()),
        out_shape=(list_shape, list_shape, jax.ShapeDtypeStruct((2,), jnp.int32)),
        cost_estimate=pl.CostEstimate(flops=10**7, transcendentals=0, bytes_accessed=10**4),
        name="pairlist",
    )(active, jnp.asarray(codes))

    add_np, scale_np = shift_tables()
    add_tab = jnp.asarray(add_np, jnp.bfloat16)
    scale_tab = jnp.asarray(scale_np, jnp.bfloat16)

    ones = jnp.ones_like(radius)
    zeros = jnp.zeros_like(radius)
    length = disc_pos[0] * disc_pos[0] + disc_pos[1] * disc_pos[1] + 0.5 * SOFTEN
    state = jnp.stack([disc_pos[0], disc_pos[1], length, ones, radius, ones, zeros, zeros], axis=2)
    over_mass = 1.0 / ((radius / 0.06) ** 2)
    vel = jnp.stack([disc_vel[0], disc_vel[1], over_mass] + [zeros] * 5, axis=2)
    vel = vel.reshape(block_count, 8, disc_count)
    bonds = bond_list.reshape(BONDS, block_count, disc_count)
    near_scratch = [
        pltpu.VMEM((block_count + 1, 48, 4 * disc_count), jnp.bfloat16),
        pltpu.VMEM((block_count + 1, 32, 3 * disc_count), jnp.bfloat16),
    ]
    acc_shape = (block_count + 1, 16, disc_count)

    def substep(state, vel):
        state, left, right, low, high = halos(state)
        own = state.reshape(block_count, 8, disc_count)
        inner = pl.pallas_call(
            inner_kernel,
            in_specs=[smem(), smem()] + [vmem()] * 3,
            out_specs=vmem(),
            out_shape=jax.ShapeDtypeStruct(acc_shape, f32),
            scratch_shapes=[pltpu.VMEM((block_count, disc_count, DEPTH), jnp.bfloat16)]
            + near_scratch,
            cost_estimate=pl.CostEstimate(
                flops=8 * 10**9, transcendentals=10**7, bytes_accessed=2 * 10**6
            ),
            name="inner",
        )(pair_count, inner_list, own, add_tab, scale_tab)
        own, vel = pl.pallas_call(
            outer_kernel,
            in_specs=[smem(), smem()] + [vmem()] * 10,
            out_specs=(vmem(), vmem()),
            out_shape=(
                jax.ShapeDtypeStruct(own.shape, f32),
                jax.ShapeDtypeStruct(own.shape, f32),
            ),
            scratch_shapes=[
                pltpu.VMEM((wide_count - block_count + 1, disc_count, DEPTH), jnp.bfloat16)
            ]
            + near_scratch
            + [pltpu.VMEM(acc_shape, f32)],
            cost_estimate=pl.CostEstimate(
                flops=10**9, transcendentals=10**6, bytes_accessed=4 * 10**6
            ),
            name="outer",
        )(
            pair_count,
            outer_list,
            own,
            left,
            right,
            low,
            high,
            vel,
            bonds,
            add_tab,
            scale_tab,
            inner,
        )
        return own.reshape(rows_dev, cols_dev, 8, disc_count), vel

    state, vel = substep(state, vel)
    state, west, east, from_south, from_north, tops = lax.optimization_barrier(
        (state, west, east, from_south, from_north, tops)
    )

    is_top = (lax.axis_index("gy") == lat_tiles - 1).astype(jnp.int32).reshape(1)
    latitude = (lax.axis_index("gy") * tile_rows + jnp.arange(tile_rows, dtype=jnp.int32)).astype(
        f32
    )
    coriolis = SPIN_RATE * (2.0 * (latitude + 0.5) / (tile_rows * lat_tiles) - 1.0)
    coriolis = jnp.broadcast_to(coriolis[:, None], (tile_rows, tile_cols))
    chunk = next(size for size in (6, 4, 3, 2, 1) if layers % size == 0)

    def whole(shape):
        return pl.BlockSpec(shape, lambda g: (0,) * len(shape))

    def layer_block(size, index):
        return pl.BlockSpec(
            (fields, size, tile_rows, tile_cols), lambda g: (0, index(g), 0, 0)
        )

    updated = pl.pallas_call(
        ocean_kernel,
        grid=(layers // chunk,),
        in_specs=[
            smem(),
            layer_block(chunk, lambda g: g),
            layer_block(1, lambda g: jnp.maximum(g * chunk - 1, 0)),
            layer_block(1, lambda g: jnp.minimum(g * chunk + chunk, layers - 1)),
            pl.BlockSpec((chunk, tile_rows, tile_cols), lambda g: (g, 0, 0)),
            whole(west.shape),
            whole(east.shape),
            whole(from_south.shape),
            whole(from_north.shape),
            whole(tops.shape),
            whole((1, tile_cols)),
            whole(coriolis.shape),
        ],
        out_specs=layer_block(chunk, lambda g: g),
        out_shape=jax.ShapeDtypeStruct(ocean_state.shape, f32),
        scratch_shapes=[
            pltpu.VMEM((planes, tile_cols), f32),
            pltpu.VMEM((tile_cols, tile_cols), f32),
            pltpu.VMEM((tile_cols, tile_cols), f32),
        ],
        cost_estimate=pl.CostEstimate(flops=10**8, transcendentals=0, bytes_accessed=7 * 10**6),
        name="ocean",
    )(
        is_top,
        ocean_state,
        ocean_state,
        ocean_state,
        mix_coef,
        west,
        east,
        from_south,
        from_north,
        tops,
        fold_perm.reshape(1, tile_cols),
        coriolis,
    )

    cells = remap_cell[0].reshape(-1)
    surface = updated[0:2, 0].reshape(2, tile_rows * tile_cols)
    unforced = jnp.take(surface, cells, axis=1).reshape(2, tile_count, capacity)
    early = jnp.concatenate(
        [
            jnp.broadcast_to(cells.astype(f32)[None], (tile_count, slots)),
            unforced.transpose(1, 0, 2).reshape(tile_count, 2 * capacity),
        ],
        axis=1,
    )
    early = lax.all_to_all(early, ("gx", "gy"), split_axis=0, concat_axis=0, tiled=True)
    for step in range(1, SUB):
        state, vel = substep(state, vel)
        if step == 1:
            state, early = lax.optimization_barrier((state, early))
    all_cells = early[:, :slots].reshape(tile_count, tile_count, capacity)
    unforced = early[:, slots:].reshape(tile_count, 2, capacity)

    vel_rows = vel[:, 0:2]
    weight = radius.reshape(block_count, 1, disc_count) ** 2
    impulse = DRAG_ICE * jnp.sum(weight * vel_rows, axis=-1)
    selector = (
        remap_block[0].reshape(-1)[:, None] == jnp.arange(block_count, dtype=jnp.int32)[None]
    ).astype(f32)
    outgoing = lax.dot_general(
        impulse, selector, (((0,), (1,)), ((), ())), precision=HIGHEST
    ).reshape(1, 2 * slots)
    arrived = lax.all_to_all(
        jnp.broadcast_to(outgoing, (tile_count, 2 * slots)),
        ("gx", "gy"),
        split_axis=0,
        concat_axis=0,
        tiled=True,
    ).reshape(tile_count, 2, tile_count, capacity)

    tile_id = lax.axis_index("gx") * lat_tiles + lax.axis_index("gy")
    mine = lax.dynamic_index_in_dim(all_cells, tile_id, axis=1, keepdims=False)
    same = all_cells[:, None] == mine[:, :, None, None]
    landed = arrived.transpose(1, 2, 0, 3)
    forced = jnp.sum(jnp.where(same[None], landed[:, :, None], 0.0), axis=(3, 4))
    current = unforced.transpose(1, 0, 2) + forced
    per_block = jnp.dot(current.reshape(2, slots), selector, precision=HIGHEST)
    per_block = per_block.reshape(2, rows_dev, cols_dev)
    velocity = vel.reshape(rows_dev, cols_dev, 8, disc_count)[:, :, 0:2].transpose(2, 0, 1, 3)
    position = state[:, :, 0:2].transpose(2, 0, 1, 3)
    vel_next = velocity + DRAG_BACK * (per_block[..., None] - velocity)

    here = lax.dynamic_index_in_dim(arrived, tile_id, axis=2, keepdims=False)
    here = here.transpose(1, 0, 2).reshape(2, 1, slots)
    in_row = (cells // tile_cols)[None] == jnp.arange(tile_rows, dtype=jnp.int32)[:, None]
    in_col = (cells % tile_cols)[:, None] == jnp.arange(tile_cols, dtype=jnp.int32)[None]
    forcing = jnp.dot(
        jnp.where(in_row[None], here, 0.0).reshape(2 * tile_rows, slots),
        in_col.astype(f32),
        precision=HIGHEST,
    ).reshape(2, tile_rows, tile_cols)
    updated = updated.at[0:2, 0].add(forcing)
    return (position, vel_next, updated)


def solution(mesh):
    in_specs = (
        P(None, "gy", "gx", None),
        P(None, "gy", "gx", None),
        P("gy", "gx", None),
        P(None, "gy", "gx", None),
        P(None, "gy", "gx"),
        P(("gx", "gy"), None, None),
        P(None, None, "gy", "gx"),
        P(None, "gy", "gx"),
        P(("gx", "gy"), None, None),
        P("gx"),
    )
    out_specs = (P(None, "gy", "gx", None), P(None, "gy", "gx", None), P(None, None, "gy", "gx"))
    return jax.shard_map(body, mesh=mesh, in_specs=in_specs, out_specs=out_specs, check_vma=False)
```

time: 532 us -> 241 us (0.45)
  other arithmetic: 313 us -> 3.87 us
  Pallas kernels: 0 us -> 152 us
  matrix products: 91 us -> 2.28 us
  local copies, waits for them, and re-layouts: 45.7 us -> 22 us
  blocking collectives: 13.6 us -> 0 us
  waiting for transfers between devices: 15.2 us -> 8.3 us
    reduce_sum x6 -> x2, other arithmetic: 282 us -> 2.38 us  [the longest x1 1.25 us: body(): impulse = DRAG_ICE * jnp.sum(weight * vel_rows, axis=-1)]
    pallas_call x0 -> x9, Pallas kernels: none -> 152 us  [the longest x3 94.4 us: substep(): pl.pallas_call(inner_kernel, in_specs=[smem(), smem()] + [vmem()] * 3, ou...]
    dot_general x6 -> x3, matrix products: 91 us -> 2.28 us  [the longest x1 1.63 us: body(): jnp.dot(jnp.where(in_row[None], here, 0.0).reshape(2 * tile_rows, slots),...]
    all_gather x1 -> x0, blocking collectives: 13.6 us -> none  [body(): piece = lax.all_gather(top_row, 'gx', axis=2, tiled=True)]
    slice x10 -> x12, local copies, waits for them, and re-layouts: 16.5 us -> 4.7 us  [the longest x1 1.08 us: body(): position = state[:, :, 0:2].transpose(2, 0, 1, 3)]
    all_to_all x2 -> x3, starting transfers between devices: 7.61 us -> 17 us  [the longest x1 6.97 us: body(): lax.all_to_all(early, ('gx', 'gy'), split_axis=0, concat_axis=0, tiled=True)]
    ppermute x2 -> x0, local copies, waits for them, and re-layouts: 8.68 us -> none  [the longest x1 4.36 us: with_halo(): lax.ppermute(lax.slice_in_dim(block, 0, width, axis=dim), axis, backward)]
    all_to_all x2 -> x3, waiting for transfers between devices: 12.2 us -> 4.33 us  [the longest x1 4.32 us: body(): lax.all_to_all(jnp.broadcast_to(outgoing, (tile_count, 2 * slots)), ('gx'...]
  transfers between devices with their start and end apart: 18 -> 19, of which waited for: 5 -> 3; matrix products, arithmetic and copies ran while one was open for 60% -> 5% of each run, Pallas kernels for 0% -> 53%
where the time goes in v1:
time: 241 us; the launch traced here: 240 us
  Pallas kernels  152 us (63%)
  starting transfers between devices  50 us (21%)
  local copies, waits for them, and re-layouts  22 us (9%)
  waiting for transfers between devices  8.3 us (3%)
  other arithmetic  3.87 us (2%)
    pallas_call x3, Pallas kernels, substep(): pl.pallas_call(inner_kernel, in_specs=[smem(), smem()] + [vmem()] * 3, ou...  94.4 us
    pallas_call x3, Pallas kernels, substep(): pl.pallas_call(outer_kernel, in_specs=[smem(), smem()] + [vmem()] * 10, o...  36.6 us
    ppermute x3, starting transfers between devices, halos(): low = lax.ppermute(top, 'gy', line('gy', 1))  14.6 us
    pallas_call x1, Pallas kernels, body(): pl.pallas_call(ocean_kernel, grid=(layers // chunk,), in_specs=[smem(), l...  9.46 us
    pallas_call x1, Pallas kernels, body(): pl.pallas_call(functools.partial(list_kernel, own=block_count), in_specs=...  7.02 us
    all_to_all x1, starting transfers between devices, body(): lax.all_to_all(early, ('gx', 'gy'), split_axis=0, concat_axis=0, tiled=True)  6.97 us
    ppermute x3, starting transfers between devices, halos(): right = lax.ppermute(state[:, 0], 'gx', ring('gx', -1))  6.06 us
    all_to_all x1, starting transfers between devices, body(): lax.all_to_all(jnp.broadcast_to(outgoing, (tile_count, 2 * slots)), ('gx'...  5.77 us
  transfers between devices with their start and end apart: 19, of which 3 were waited for; matrix products, arithmetic and copies ran while one was open for 5% of the time, Pallas kernels for 53%

profile of v1, /device:TPU:0, one launch (start us, length us, event | category | flops | bytes accessed | tf_op | source)
XLA Modules:
  0.0 239.8 jit_solution(8170055689601746241)
XLA Ops:
  3.4 3.4 %collective-permute-start.1 = (f32[8,8,128]{2,1,0:T(8,128)S(1)}, f32[8,8,128]{2,1,0:T(8,128)S(1)}, u32[]{:S(2)}, u32[]{:S(2)}) collective-permute-start(f32[8,8,128]{2,1,0:T(8,128)S(1)} %get-tuple-element.84), channel_id=1, source_target_pairs={{0,28},{4,0},{8,4},{12,8},{16,12},{20,16},{24,20},{28,24},{1,29},{... | collective-permute-start | bytes 98312 | tf_op jit(solution)/shard_map/ppermute | solution.py:395
  6.8 4.6 %edges.1 = (f32[128,128]{1,0:T(8,128)}, f32[192,128]{1,0:T(8,128)}, f32[192,128]{1,0:T(8,128)}) custom-call(f32[6144,128]{1,0:T(8,128)} %bitcast.91), custom_call_target="tpu_custom_call" | custom-call | flops 10000000 | bytes 4000000 | tf_op jit(solution)/shard_map/edges/pallas_call | solution.py:427
  12.3 3.5 %collective-permute-start.6 = (f32[192,128]{1,0:T(8,128)}, f32[192,128]{1,0:T(8,128)S(1)}, u32[]{:S(2)}, u32[]{:S(2)}) collective-permute-start(f32[192,128]{1,0:T(8,128)} %get-tuple-element.52), channel_id=1, source_target_pairs={{0,1},{1,2},{2,3},{4,5},{5,6},{6,7},{8,9},{9,10},{10,11},{12,13},{... | collective-permute-start | bytes 294920 | tf_op jit(solution)/shard_map/ppermute | solution.py:439
  15.8 1.3 collective-permute-start.7
  17.1 1.9 broadcast_in_dim.103
  19.0 4.3 %all-to-all-start = ((f32[8,192,128]{2,1,0:T(8,128)}), f32[8,192,128]{2,1,0:T(8,128)S(1)}, u32[]{:S(2)}, u32[]{:S(2)}) async-start(f32[8,192,128]{2,1,0:T(8,128)} %broadcast_in_dim.103), calls=%async_computation | async-start | bytes 1572864 | tf_op jit(solution)/shard_map/all_to_all | solution.py:442
  24.8 1.2 stack.30.vel_ref
  26.1 7.0 %pairlist.1 = (s32[1168]{0:T(1024)}, s32[1168]{0:T(1024)}, s32[2]{0:T(128)}) custom-call(s32[1024]{0:T(1024)} %reshape.353.active_ref, s32[1152]{0:T(1024)} %constant.139.clone.code_ref), custom_call_target="tpu_custom_call" | custom-call | flops 10000000 | bytes 10000 | tf_op jit(solution)/shard_map/pairlist/pallas_call | solution.py:457
  34.0 4.5 %collective-permute-start.2 = (f32[18,8,128]{2,1,0:T(8,128)S(1)}, f32[18,8,128]{2,1,0:T(8,128)S(1)}, u32[]{:S(2)}, u32[]{:S(2)}) collective-permute-start(f32[18,8,128]{2,1,0:T(8,128)S(1)} %get-tuple-element.47), channel_id=1, source_target_pairs={{0,1},{1,2},{2,3},{4,5},{5,6},{6,7},{8,9},{9,10},{10,11},{12,13},{... | collective-permute-start | bytes 221192 | tf_op jit(solution)/shard_map/ppermute | solution.py:399
  38.6 1.3 collective-permute-start.3
  39.9 31.4 %inner.3.inner_ref = f32[129,16,128]{2,1,0:T(8,128)} custom-call(s32[2]{0:T(128)} %get-tuple-element.44.count_ref, s32[1168]{0:T(1024)} %get-tuple-element.49.list_ref, f32[128,8,128]{2,1,0:T(8,128)} %bitcast.101, bf16[9,32,384]{2,1,0:T(8,128)(2,1)} %constant.140.clone.add_ref, bf16[9,32,128]{2,1,0:T(8,128)(2,1)} %constant.141.clone.scale_ref), custom_call_target="tpu_custom_call" | custom-call | flops 8000000000 | bytes 2000000 | tf_op jit(solution)/shard_map/inner/pallas_call | solution.py:487
  71.3 3.1 %collective-permute-start.5 = (f32[64,128]{1,0:T(8,128)S(1)}, f32[64,128]{1,0:T(8,128)S(1)}, u32[]{:S(2)}, u32[]{:S(2)}) collective-permute-start(f32[64,128]{1,0:T(8,128)S(1)} %get-tuple-element.91), channel_id=1, source_target_pairs={{0,28},{4,0},{8,4},{12,8},{16,12},{20,16},{24,20},{28,24},{1,29},{... | collective-permute-start | bytes 98312 | tf_op jit(solution)/shard_map/ppermute | solution.py:438
  75.1 12.1 %outer.3 = (f32[128,8,128]{2,1,0:T(8,128)}, f32[128,8,128]{2,1,0:T(8,128)}) custom-call(s32[2]{0:T(128)} %get-tuple-element.44.count_ref, s32[1168]{0:T(1024)} %get-tuple-element.45.list_ref, f32[128,8,128]{2,1,0:T(8,128)} %bitcast.102, f32[8,8,128]{2,1,0:T(8,128)} %copy-done.11, f32[8,8,128]{2,1,0:T(8,128)} %copy-done.10, f32[18,8,128]{2,1,0:T(8,128)} %copy-done.18, ...), custom_call_target="tpu_custom_call" | custom-call | flops 1000000000 | bytes 4000000 | tf_op jit(solution)/shard_map/outer/pallas_call | solution.py:499
  90.3 9.5 %ocean.1 = f32[4,48,32,128]{3,2,1,0:T(8,128)} custom-call(s32[1]{0:T(128)} %bitcast.21.flags_ref, f32[4,48,32,128]{3,2,1,0:T(8,128)} %after_ref.1, f32[4,48,32,128]{3,2,1,0:T(8,128)} %after_ref.1, f32[4,48,32,128]{3,2,1,0:T(8,128)} %after_ref.1, f32[48,32,128]{2,1,0:T(8,128)} %mix_ref.1, f32[64,128]{1,0:T(8,128)} %copy-done.5, f32[64,128]{1,0:T(8,128)} %copy-done.6, ...), custom_call_target="tpu_custom_call" | custom-call | flops 100000000 | bytes 7000000 | tf_op jit(solution)/shard_map/ocean/pallas_call | solution.py:553
  102.8 7.0 %all-to-all-start.1 = ((f32[32,1,272]{2,1,0:T(1,128)}), f32[32,1,272]{2,1,0:T(1,128)S(1)}, u32[]{:S(2)}, u32[]{:S(2)}) async-start(f32[32,1,272]{2,1,0:T(1,128)} %all_to_all.16), calls=%async_computation.1 | async-start | bytes 98304 | tf_op jit(solution)/shard_map/all_to_all | solution.py:604
  109.9 3.7 %collective-permute-start.10 = (f32[18,8,128]{2,1,0:T(8,128)S(1)}, f32[18,8,128]{2,1,0:T(8,128)S(1)}, u32[]{:S(2)}, u32[]{:S(2)}) collective-permute-start(f32[18,8,128]{2,1,0:T(8,128)S(1)} %pad_maximum_fusion.3), channel_id=1, source_target_pairs={{0,1},{1,2},{2,3},{4,5},{5,6},{6,7},{8,9},{9,10},{10,11},{12,13},{... | collective-permute-start | bytes 221192 | tf_op jit(solution)/shard_map/ppermute | solution.py:399
  113.6 1.3 collective-permute-start.11
  114.9 31.5 %inner.4.inner_ref = f32[129,16,128]{2,1,0:T(8,128)} custom-call(s32[2]{0:T(128)} %get-tuple-element.44.count_ref, s32[1168]{0:T(1024)} %get-tuple-element.49.list_ref, f32[128,8,128]{2,1,0:T(8,128)} %get-tuple-element.50, bf16[9,32,384]{2,1,0:T(8,128)(2,1)} %constant.140.clone.add_ref, bf16[9,32,128]{2,1,0:T(8,128)(2,1)} %constant.141.clone.scale_ref), custom_call_target="tpu_custom_call" | custom-call | flops 8000000000 | bytes 2000000 | tf_op jit(solution)/shard_map/inner/pallas_call | solution.py:487
  147.1 12.1 %outer.4 = (f32[128,8,128]{2,1,0:T(8,128)}, f32[128,8,128]{2,1,0:T(8,128)}) custom-call(s32[2]{0:T(128)} %get-tuple-element.44.count_ref, s32[1168]{0:T(1024)} %get-tuple-element.45.list_ref, f32[128,8,128]{2,1,0:T(8,128)} %get-tuple-element.50, f32[8,8,128]{2,1,0:T(8,128)} %copy-done.13, f32[8,8,128]{2,1,0:T(8,128)} %copy-done.12, ...), custom_call_target="tpu_custom_call" | custom-call | flops 1000000000 | bytes 4000000 | tf_op jit(solution)/shard_map/outer/pallas_call | solution.py:499
  161.0 2.6 %collective-permute-start.13 = (f32[8,8,128]{2,1,0:T(8,128)S(1)}, f32[8,8,128]{2,1,0:T(8,128)S(1)}, u32[]{:S(2)}, u32[]{:S(2)}) collective-permute-start(f32[8,8,128]{2,1,0:T(8,128)S(1)} %get-tuple-element.76), channel_id=1, source_target_pairs={{0,28},{4,0},{8,4},{12,8},{16,12},{20,16},{24,20},{28,24},{1,29},{... | collective-permute-start | bytes 98312 | tf_op jit(solution)/shard_map/ppermute | solution.py:395
  163.8 1.3 collective-permute-done.13.right_ref
  165.1 2.6 %collective-permute-done.12.left_ref = f32[8,8,128]{2,1,0:T(8,128)S(1)} collective-permute-done((f32[8,8,128]{2,1,0:T(8,128)S(1)}, f32[8,8,128]{2,1,0:T(8,128)S(1)}, u32[]{:S(2)}, u32[]{:S(2)}) %collective-permute-start.12) | collective-permute-done | bytes 32800 | tf_op jit(solution)/shard_map/ppermute | solution.py:394
  167.8 6.4 %collective-permute-start.14 = (f32[18,8,128]{2,1,0:T(8,128)S(1)}, f32[18,8,128]{2,1,0:T(8,128)S(1)}, u32[]{:S(2)}, u32[]{:S(2)}) collective-permute-start(f32[18,8,128]{2,1,0:T(8,128)S(1)} %pad_maximum_fusion.5), channel_id=1, source_target_pairs={{0,1},{1,2},{2,3},{4,5},{5,6},{6,7},{8,9},{9,10},{10,11},{12,13},{... | collective-permute-start | bytes 221192 | tf_op jit(solution)/shard_map/ppermute | solution.py:399
  174.2 1.3 collective-permute-start.15
  175.5 31.5 %inner.5.inner_ref = f32[129,16,128]{2,1,0:T(8,128)} custom-call(s32[2]{0:T(128)} %get-tuple-element.44.count_ref, s32[1168]{0:T(1024)} %get-tuple-element.49.list_ref, f32[128,8,128]{2,1,0:T(8,128)} %get-tuple-element.59, bf16[9,32,384]{2,1,0:T(8,128)(2,1)} %constant.140.clone.add_ref, bf16[9,32,128]{2,1,0:T(8,128)(2,1)} %constant.141.clone.scale_ref), custom_call_target="tpu_custom_call" | custom-call | flops 8000000000 | bytes 2000000 | tf_op jit(solution)/shard_map/inner/pallas_call | solution.py:487
  207.6 12.3 %outer.5 = (f32[128,8,128]{2,1,0:T(8,128)}, f32[128,8,128]{2,1,0:T(8,128)}) custom-call(s32[2]{0:T(128)} %get-tuple-element.44.count_ref, s32[1168]{0:T(1024)} %get-tuple-element.45.list_ref, f32[128,8,128]{2,1,0:T(8,128)} %get-tuple-element.59, f32[8,8,128]{2,1,0:T(8,128)} %copy-done.15, f32[8,8,128]{2,1,0:T(8,128)} %copy-done.14, ...), custom_call_target="tpu_custom_call" | custom-call | flops 1000000000 | bytes 4000000 | tf_op jit(solution)/shard_map/outer/pallas_call | solution.py:499
  220.0 1.3 multiply_reduce_fusion
  222.2 5.8 %all-to-all-start.2 = ((f32[32,1,512]{2,1,0:T(1,128)}), f32[32,1,512]{2,1,0:T(1,128)S(1)}, u32[]{:S(2)}, u32[]{:S(2)}) async-start(f32[32,1,512]{2,1,0:T(1,128)} %broadcast_in_dim.110), calls=%async_computation.2 | async-start | bytes 131072 | tf_op jit(solution)/shard_map/all_to_all | solution.py:621
  228.3 1.1 slice.200
  231.1 4.3 %all-to-all-done.2 = f32[32,1,512]{2,1,0:T(1,128)S(1)} async-done(((f32[32,1,512]{2,1,0:T(1,128)}), f32[32,1,512]{2,1,0:T(1,128)S(1)}, u32[]{:S(2)}, u32[]{:S(2)}) %all-to-all-start.2) | async-done | bytes 65568 | tf_op jit(solution)/shard_map/all_to_all | solution.py:621
  235.6 1.1 select_reduce_fusion
  238.2 1.6 fusion.1
  (146 shorter events, 20.6 us)
Async XLA Ops:
  3.4 29.7 %collective-permute-start.1 = (f32[8,8,128]{2,1,0:T(8,128)S(1)}, f32[8,8,128]{2,1,0:T(8,128)S(1)}, u32[]{:S(2)}, u32[]{:S(2)}) collective-permute-start(f32[8,8,128]{2,1,0:T(8,128)S(1)} %get-tuple-element.84), channel_id=1, source_target_pairs={{0,28},{4,0},{8,4},{12,8},{16,12},{20,16},{24,20},{28,24},{1,29},{... | collective-permute-start | bytes 98312 | tf_op jit(solution)/shard_map/ppermute | solution.py:395
  6.8 26.3 %collective-permute-start = (f32[8,8,128]{2,1,0:T(8,128)S(1)}, f32[8,8,128]{2,1,0:T(8,128)S(1)}, u32[]{:S(2)}, u32[]{:S(2)}) collective-permute-start(f32[8,8,128]{2,1,0:T(8,128)S(1)} %get-tuple-element.83), channel_id=1, source_target_pairs={{0,4},{4,8},{8,12},{12,16},{16,20},{20,24},{24,28},{28,0},{1,5},{5... | collective-permute-start | bytes 98312 | tf_op jit(solution)/shard_map/ppermute | solution.py:394
  11.4 11.9 %copy-start.1 = (f32[8,16,128]{2,1,0:T(8,128)S(1)}, f32[8,16,128]{2,1,0:T(8,128)}, u32[]{:S(2)}) copy-start(f32[8,16,128]{2,1,0:T(8,128)} %param.18) | copy-start | bytes 196612
  11.4 11.9 %copy-start.8 = (s32[1,32,8]{1,2,0:T(8,128)S(1)}, s32[1,32,8]{1,2,0:T(8,128)}, u32[]{:S(2)}) copy-start(s32[1,32,8]{1,2,0:T(8,128)} %param.24) | copy-start | bytes 3076
  11.4 12.2 %copy-start.2 = (f32[2,8,16,128]{3,2,1,0:T(8,128)S(1)}, f32[2,8,16,128]{3,2,1,0:T(8,128)}, u32[]{:S(2)}) copy-start(f32[2,8,16,128]{3,2,1,0:T(8,128)} %param.17) | copy-start | bytes 393220
  11.4 12.3 %copy-start.16 = (s32[8]{0:T(128)S(1)}, s32[8]{0:T(128)}, u32[]{:S(2)}) copy-start(s32[8]{0:T(128)} %constant.138.clone) | copy-start | bytes 100
  11.4 12.4 %copy-start.7 = (s32[8,8,16]{2,1,0:T(8,128)S(1)}, s32[8,8,16]{2,1,0:T(8,128)}, u32[]{:S(2)}) copy-start(s32[8,8,16]{2,1,0:T(8,128)} %param.20) | copy-start | bytes 12292
  11.4 13.1 %copy-start.9 = (s32[1,32,8]{1,2,0:T(8,128)S(1)}, s32[1,32,8]{1,2,0:T(8,128)}, u32[]{:S(2)}) copy-start(s32[1,32,8]{1,2,0:T(8,128)} %param.21) | copy-start | bytes 3076
  12.3 74.9 %collective-permute-start.4 = (f32[64,128]{1,0:T(8,128)S(1)}, f32[64,128]{1,0:T(8,128)S(1)}, u32[]{:S(2)}, u32[]{:S(2)}) collective-permute-start(f32[64,128]{1,0:T(8,128)S(1)} %get-tuple-element.92), channel_id=1, source_target_pairs={{0,4},{4,8},{8,12},{12,16},{16,20},{20,24},{24,28},{28,0},{1,5},{5... | collective-permute-start | bytes 98312 | tf_op jit(solution)/shard_map/ppermute | solution.py:437
  12.3 74.9 %collective-permute-start.6 = (f32[192,128]{1,0:T(8,128)}, f32[192,128]{1,0:T(8,128)S(1)}, u32[]{:S(2)}, u32[]{:S(2)}) collective-permute-start(f32[192,128]{1,0:T(8,128)} %get-tuple-element.52), channel_id=1, source_target_pairs={{0,1},{1,2},{2,3},{4,5},{5,6},{6,7},{8,9},{9,10},{10,11},{12,13},{... | collective-permute-start | bytes 294920 | tf_op jit(solution)/shard_map/ppermute | solution.py:439
  15.8 71.5 %collective-permute-start.7 = (f32[192,128]{1,0:T(8,128)}, f32[192,128]{1,0:T(8,128)S(1)}, u32[]{:S(2)}, u32[]{:S(2)}) collective-permute-start(f32[192,128]{1,0:T(8,128)} %get-tuple-element.53), channel_id=1, source_target_pairs={{1,0},{2,1},{3,2},{5,4},{6,5},{7,6},{9,8},{10,9},{11,10},{13,12},{... | collective-permute-start | bytes 294920 | tf_op jit(solution)/shard_map/ppermute | solution.py:440
  19.0 68.3 %all-to-all-start = ((f32[8,192,128]{2,1,0:T(8,128)}), f32[8,192,128]{2,1,0:T(8,128)S(1)}, u32[]{:S(2)}, u32[]{:S(2)}) async-start(f32[8,192,128]{2,1,0:T(8,128)} %broadcast_in_dim.103), calls=%async_computation | async-start | bytes 1572864 | tf_op jit(solution)/shard_map/all_to_all | solution.py:442
  33.1 38.2 %copy-start.10 = (f32[8,8,128]{2,1,0:T(8,128)}, f32[8,8,128]{2,1,0:T(8,128)S(1)}, u32[]{:S(2)}) copy-start(f32[8,8,128]{2,1,0:T(8,128)S(1)} %collective-permute-done.1.right_ref) | copy-start | bytes 98308
  33.1 38.1 %copy-start.11 = (f32[8,8,128]{2,1,0:T(8,128)}, f32[8,8,128]{2,1,0:T(8,128)S(1)}, u32[]{:S(2)}) copy-start(f32[8,8,128]{2,1,0:T(8,128)S(1)} %collective-permute-done.left_ref) | copy-start | bytes 98308
  34.0 37.3 %collective-permute-start.2 = (f32[18,8,128]{2,1,0:T(8,128)S(1)}, f32[18,8,128]{2,1,0:T(8,128)S(1)}, u32[]{:S(2)}, u32[]{:S(2)}) collective-permute-start(f32[18,8,128]{2,1,0:T(8,128)S(1)} %get-tuple-element.47), channel_id=1, source_target_pairs={{0,1},{1,2},{2,3},{4,5},{5,6},{6,7},{8,9},{9,10},{10,11},{12,13},{... | collective-permute-start | bytes 221192 | tf_op jit(solution)/shard_map/ppermute | solution.py:399
  38.6 35.9 %collective-permute-start.3 = (f32[18,8,128]{2,1,0:T(8,128)S(1)}, f32[18,8,128]{2,1,0:T(8,128)S(1)}, u32[]{:S(2)}, u32[]{:S(2)}) collective-permute-start(f32[18,8,128]{2,1,0:T(8,128)S(1)} %get-tuple-element.48), channel_id=1, source_target_pairs={{1,0},{2,1},{3,2},{5,4},{6,5},{7,6},{9,8},{10,9},{11,10},{13,12},{... | collective-permute-start | bytes 221192 | tf_op jit(solution)/shard_map/ppermute | solution.py:400
  71.3 3.2 %copy-start.18 = (f32[18,8,128]{2,1,0:T(8,128)}, f32[18,8,128]{2,1,0:T(8,128)S(1)}, u32[]{:S(2)}) copy-start(f32[18,8,128]{2,1,0:T(8,128)S(1)} %collective-permute-done.2.low_ref) | copy-start | bytes 221188
  71.3 15.9 %collective-permute-start.5 = (f32[64,128]{1,0:T(8,128)S(1)}, f32[64,128]{1,0:T(8,128)S(1)}, u32[]{:S(2)}, u32[]{:S(2)}) collective-permute-start(f32[64,128]{1,0:T(8,128)S(1)} %get-tuple-element.91), channel_id=1, source_target_pairs={{0,28},{4,0},{8,4},{12,8},{16,12},{20,16},{24,20},{28,24},{1,29},{... | collective-permute-start | bytes 98312 | tf_op jit(solution)/shard_map/ppermute | solution.py:438
  89.1 20.7 %collective-permute-start.9 = (f32[8,8,128]{2,1,0:T(8,128)S(1)}, f32[8,8,128]{2,1,0:T(8,128)S(1)}, u32[]{:S(2)}, u32[]{:S(2)}) collective-permute-start(f32[8,8,128]{2,1,0:T(8,128)S(1)} %get-tuple-element.80), channel_id=1, source_target_pairs={{0,28},{4,0},{8,4},{12,8},{16,12},{20,16},{24,20},{28,24},{1,29},{... | collective-permute-start | bytes 98312 | tf_op jit(solution)/shard_map/ppermute | solution.py:395
  89.1 20.7 %collective-permute-start.8 = (f32[8,8,128]{2,1,0:T(8,128)S(1)}, f32[8,8,128]{2,1,0:T(8,128)S(1)}, u32[]{:S(2)}, u32[]{:S(2)}) collective-permute-start(f32[8,8,128]{2,1,0:T(8,128)S(1)} %get-tuple-element.79), channel_id=1, source_target_pairs={{0,4},{4,8},{8,12},{12,16},{16,20},{20,24},{24,28},{28,0},{1,5},{5... | collective-permute-start | bytes 98312 | tf_op jit(solution)/shard_map/ppermute | solution.py:394
  102.8 43.6 %all-to-all-start.1 = ((f32[32,1,272]{2,1,0:T(1,128)}), f32[32,1,272]{2,1,0:T(1,128)S(1)}, u32[]{:S(2)}, u32[]{:S(2)}) async-start(f32[32,1,272]{2,1,0:T(1,128)} %all_to_all.16), calls=%async_computation.1 | async-start | bytes 98304 | tf_op jit(solution)/shard_map/all_to_all | solution.py:604
  109.8 36.6 %copy-start.12 = (f32[8,8,128]{2,1,0:T(8,128)}, f32[8,8,128]{2,1,0:T(8,128)S(1)}, u32[]{:S(2)}) copy-start(f32[8,8,128]{2,1,0:T(8,128)S(1)} %collective-permute-done.9.right_ref) | copy-start | bytes 98308
  109.8 36.5 %copy-start.13 = (f32[8,8,128]{2,1,0:T(8,128)}, f32[8,8,128]{2,1,0:T(8,128)S(1)}, u32[]{:S(2)}) copy-start(f32[8,8,128]{2,1,0:T(8,128)S(1)} %collective-permute-done.8.left_ref) | copy-start | bytes 98308
  109.9 36.6 %collective-permute-start.10 = (f32[18,8,128]{2,1,0:T(8,128)S(1)}, f32[18,8,128]{2,1,0:T(8,128)S(1)}, u32[]{:S(2)}, u32[]{:S(2)}) collective-permute-start(f32[18,8,128]{2,1,0:T(8,128)S(1)} %pad_maximum_fusion.3), channel_id=1, source_target_pairs={{0,1},{1,2},{2,3},{4,5},{5,6},{6,7},{8,9},{9,10},{10,11},{12,13},{... | collective-permute-start | bytes 221192 | tf_op jit(solution)/shard_map/ppermute | solution.py:399
  113.6 32.9 %collective-permute-start.11 = (f32[18,8,128]{2,1,0:T(8,128)S(1)}, f32[18,8,128]{2,1,0:T(8,128)S(1)}, u32[]{:S(2)}, u32[]{:S(2)}) collective-permute-start(f32[18,8,128]{2,1,0:T(8,128)S(1)} %pad_maximum_fusion.2), channel_id=1, source_target_pairs={{1,0},{2,1},{3,2},{5,4},{6,5},{7,6},{9,8},{10,9},{11,10},{13,12},{... | collective-permute-start | bytes 221192 | tf_op jit(solution)/shard_map/ppermute | solution.py:400
  161.0 4.2 %collective-permute-start.13 = (f32[8,8,128]{2,1,0:T(8,128)S(1)}, f32[8,8,128]{2,1,0:T(8,128)S(1)}, u32[]{:S(2)}, u32[]{:S(2)}) collective-permute-start(f32[8,8,128]{2,1,0:T(8,128)S(1)} %get-tuple-element.76), channel_id=1, source_target_pairs={{0,28},{4,0},{8,4},{12,8},{16,12},{20,16},{24,20},{28,24},{1,29},{... | collective-permute-start | bytes 98312 | tf_op jit(solution)/shard_map/ppermute | solution.py:395
  163.5 4.2 %collective-permute-start.12 = (f32[8,8,128]{2,1,0:T(8,128)S(1)}, f32[8,8,128]{2,1,0:T(8,128)S(1)}, u32[]{:S(2)}, u32[]{:S(2)}) collective-permute-start(f32[8,8,128]{2,1,0:T(8,128)S(1)} %get-tuple-element.75), channel_id=1, source_target_pairs={{0,4},{4,8},{8,12},{12,16},{16,20},{20,24},{24,28},{28,0},{1,5},{5... | collective-permute-start | bytes 98312 | tf_op jit(solution)/shard_map/ppermute | solution.py:394
  165.1 41.8 %copy-start.14 = (f32[8,8,128]{2,1,0:T(8,128)}, f32[8,8,128]{2,1,0:T(8,128)S(1)}, u32[]{:S(2)}) copy-start(f32[8,8,128]{2,1,0:T(8,128)S(1)} %collective-permute-done.13.right_ref) | copy-start | bytes 98308
  167.8 39.2 %copy-start.15 = (f32[8,8,128]{2,1,0:T(8,128)}, f32[8,8,128]{2,1,0:T(8,128)S(1)}, u32[]{:S(2)}) copy-start(f32[8,8,128]{2,1,0:T(8,128)S(1)} %collective-permute-done.12.left_ref) | copy-start | bytes 98308
  167.8 39.2 %collective-permute-start.14 = (f32[18,8,128]{2,1,0:T(8,128)S(1)}, f32[18,8,128]{2,1,0:T(8,128)S(1)}, u32[]{:S(2)}, u32[]{:S(2)}) collective-permute-start(f32[18,8,128]{2,1,0:T(8,128)S(1)} %pad_maximum_fusion.5), channel_id=1, source_target_pairs={{0,1},{1,2},{2,3},{4,5},{5,6},{6,7},{8,9},{9,10},{10,11},{12,13},{... | collective-permute-start | bytes 221192 | tf_op jit(solution)/shard_map/ppermute | solution.py:399
  174.2 32.8 %collective-permute-start.15 = (f32[18,8,128]{2,1,0:T(8,128)S(1)}, f32[18,8,128]{2,1,0:T(8,128)S(1)}, u32[]{:S(2)}, u32[]{:S(2)}) collective-permute-start(f32[18,8,128]{2,1,0:T(8,128)S(1)} %pad_maximum_fusion.4), channel_id=1, source_target_pairs={{1,0},{2,1},{3,2},{5,4},{6,5},{7,6},{9,8},{10,9},{11,10},{13,12},{... | collective-permute-start | bytes 221192 | tf_op jit(solution)/shard_map/ppermute | solution.py:400
  222.2 13.3 %all-to-all-start.2 = ((f32[32,1,512]{2,1,0:T(1,128)}), f32[32,1,512]{2,1,0:T(1,128)S(1)}, u32[]{:S(2)}, u32[]{:S(2)}) async-start(f32[32,1,512]{2,1,0:T(1,128)} %broadcast_in_dim.110), calls=%async_computation.2 | async-start | bytes 131072 | tf_op jit(solution)/shard_map/all_to_all | solution.py:621
  (10 other events, 18.4 us)

commit v2 on v1

--- a/solution.py
+++ b/solution.py
@@ -22,7 +22,8 @@
 SPIN_RATE = 0.3
 ALL_SHIFTS = ((-1, -1), (-1, 0), (-1, 1), (0, -1), (0, 0), (0, 1), (1, -1), (1, 0), (1, 1))
 CENTER = 4
-UNROLL = 16
+UNROLL = 32
+OUTER_UNROLL = 16
 DEPTH = 80
 HIGHEST = lax.Precision.HIGHEST
 
@@ -152,12 +153,14 @@
     acc_ref[own] = jnp.zeros((16, 128), jnp.float32)
 
 
-def visit(count, list_ref, far_base, at_ref, head_ref, tail_ref, add_ref, scale_ref, acc_ref):
+def visit(
+    count, list_ref, far_base, at_ref, head_ref, tail_ref, add_ref, scale_ref, acc_ref, unroll
+):
     pad = jnp.zeros((32, 128), jnp.bfloat16)
 
     def pairs(step, carry):
-        for u in range(UNROLL):
-            code = list_ref[step * UNROLL + u]
+        for u in range(unroll):
+            code = list_ref[step * unroll + u]
             s = code & 15
             j = ((code >> 4) & 255) - far_base
             i = code >> 12
@@ -175,7 +178,7 @@
             acc_ref[i] = acc_ref[i] + jnp.concatenate([sum_x, sum_y], axis=0)
         return carry
 
-    lax.fori_loop(0, (count + (UNROLL - 1)) // UNROLL, pairs, 0)
+    lax.fori_loop(0, (count + (unroll - 1)) // unroll, pairs, 0)
 
 
 def inner_kernel(
@@ -192,7 +195,7 @@
     lax.fori_loop(0, own, build, 0, unroll=4)
     clear_spare(own, head_ref, tail_ref, acc_ref)
     visit(
-        count_ref[0], list_ref, 0, at_ref, head_ref, tail_ref, add_ref, scale_ref, acc_ref
+        count_ref[0], list_ref, 0, at_ref, head_ref, tail_ref, add_ref, scale_ref, acc_ref, UNROLL
     )
 
 
@@ -252,7 +255,16 @@
         lax.fori_loop(0, ref.shape[0], build_halo, 0, unroll=2)
         base = base + ref.shape[0]
     visit(
-        count_ref[1], list_ref, own, at_ref, head_ref, tail_ref, add_ref, scale_ref, acc_ref
+        count_ref[1],
+        list_ref,
+        own,
+        at_ref,
+        head_ref,
+        tail_ref,
+        add_ref,
+        scale_ref,
+        acc_ref,
+        OUTER_UNROLL,
     )
     row_id = lax.broadcasted_iota(jnp.int32, (8, 128), 0)
 

time: 241 us -> 234 us (0.971)
  starting transfers between devices: 50 us -> 45.8 us
    pallas_call x3, Pallas kernels: 94.4 us -> 89.9 us  [substep(): pl.pallas_call(inner_kernel, in_specs=[smem(), smem()] + [vmem()] * 3, ou...]
where the time goes in v2:
time: 234 us; the launch traced here: 233 us
  Pallas kernels  150 us (64%)
  starting transfers between devices  45.8 us (20%)
  local copies, waits for them, and re-layouts  22 us (9%)
  waiting for transfers between devices  8.3 us (4%)
  other arithmetic  3.87 us (2%)
    pallas_call x3, Pallas kernels, substep(): pl.pallas_call(inner_kernel, in_specs=[smem(), smem()] + [vmem()] * 3, ou...  89.9 us
    pallas_call x3, Pallas kernels, substep(): pl.pallas_call(outer_kernel, in_specs=[smem(), smem()] + [vmem()] * 10, o...  38.5 us
    ppermute x3, starting transfers between devices, halos(): low = lax.ppermute(top, 'gy', line('gy', 1))  13.4 us
    pallas_call x1, Pallas kernels, body(): pl.pallas_call(ocean_kernel, grid=(layers // chunk,), in_specs=[smem(), l...  9.46 us
    all_to_all x1, starting transfers between devices, body(): lax.all_to_all(early, ('gx', 'gy'), split_axis=0, concat_axis=0, tiled=True)  7.29 us
    pallas_call x1, Pallas kernels, body(): pl.pallas_call(functools.partial(list_kernel, own=block_count), in_specs=...  7.02 us
  transfers between devices with their start and end apart: 19, of which 3 were waited for; matrix products, arithmetic and copies ran while one was open for 5% of the time, Pallas kernels for 53%

profile of v2, /device:TPU:0, one launch (start us, length us, event | category | flops | bytes accessed | tf_op | source)
XLA Modules:
  0.0 233.1 jit_solution(7385002719103833184)
XLA Ops:
  3.4 3.4 %collective-permute-start.1 = (f32[8,8,128]{2,1,0:T(8,128)S(1)}, f32[8,8,128]{2,1,0:T(8,128)S(1)}, u32[]{:S(2)}, u32[]{:S(2)}) collective-permute-start(f32[8,8,128]{2,1,0:T(8,128)S(1)} %get-tuple-element.84), channel_id=1, source_target_pairs={{0,28},{4,0},{8,4},{12,8},{16,12},{20,16},{24,20},{28,24},{1,29},{... | collective-permute-start | bytes 98312 | tf_op jit(solution)/shard_map/ppermute | solution.py:407
  6.8 4.6 %edges.1 = (f32[128,128]{1,0:T(8,128)}, f32[192,128]{1,0:T(8,128)}, f32[192,128]{1,0:T(8,128)}) custom-call(f32[6144,128]{1,0:T(8,128)} %bitcast.91), custom_call_target="tpu_custom_call" | custom-call | flops 10000000 | bytes 4000000 | tf_op jit(solution)/shard_map/edges/pallas_call | solution.py:439
  12.3 3.5 %collective-permute-start.6 = (f32[192,128]{1,0:T(8,128)}, f32[192,128]{1,0:T(8,128)S(1)}, u32[]{:S(2)}, u32[]{:S(2)}) collective-permute-start(f32[192,128]{1,0:T(8,128)} %get-tuple-element.52), channel_id=1, source_target_pairs={{0,1},{1,2},{2,3},{4,5},{5,6},{6,7},{8,9},{9,10},{10,11},{12,13},{... | collective-permute-start | bytes 294920 | tf_op jit(solution)/shard_map/ppermute | solution.py:451
  15.8 1.3 collective-permute-start.7
  17.1 1.9 broadcast_in_dim.103
  19.0 4.3 %all-to-all-start = ((f32[8,192,128]{2,1,0:T(8,128)}), f32[8,192,128]{2,1,0:T(8,128)S(1)}, u32[]{:S(2)}, u32[]{:S(2)}) async-start(f32[8,192,128]{2,1,0:T(8,128)} %broadcast_in_dim.103), calls=%async_computation | async-start | bytes 1572864 | tf_op jit(solution)/shard_map/all_to_all | solution.py:454
  24.8 1.2 stack.30.vel_ref
  26.1 7.0 %pairlist.1 = (s32[1184]{0:T(1024)}, s32[1184]{0:T(1024)}, s32[2]{0:T(128)}) custom-call(s32[1024]{0:T(1024)} %reshape.353.active_ref, s32[1152]{0:T(1024)} %constant.139.clone.code_ref), custom_call_target="tpu_custom_call" | custom-call | flops 10000000 | bytes 10000 | tf_op jit(solution)/shard_map/pairlist/pallas_call | solution.py:469
  34.0 4.5 %collective-permute-start.2 = (f32[18,8,128]{2,1,0:T(8,128)S(1)}, f32[18,8,128]{2,1,0:T(8,128)S(1)}, u32[]{:S(2)}, u32[]{:S(2)}) collective-permute-start(f32[18,8,128]{2,1,0:T(8,128)S(1)} %get-tuple-element.47), channel_id=1, source_target_pairs={{0,1},{1,2},{2,3},{4,5},{5,6},{6,7},{8,9},{9,10},{10,11},{12,13},{... | collective-permute-start | bytes 221192 | tf_op jit(solution)/shard_map/ppermute | solution.py:411
  38.6 1.3 collective-permute-start.3
  39.9 29.9 %inner.3.inner_ref = f32[129,16,128]{2,1,0:T(8,128)} custom-call(s32[2]{0:T(128)} %get-tuple-element.44.count_ref, s32[1184]{0:T(1024)} %get-tuple-element.49.list_ref, f32[128,8,128]{2,1,0:T(8,128)} %bitcast.101, bf16[9,32,384]{2,1,0:T(8,128)(2,1)} %constant.140.clone.add_ref, bf16[9,32,128]{2,1,0:T(8,128)(2,1)} %constant.141.clone.scale_ref), custom_call_target="tpu_custom_call" | custom-call | flops 8000000000 | bytes 2000000 | tf_op jit(solution)/shard_map/inner/pallas_call | solution.py:499
  69.8 2.4 %collective-permute-start.5 = (f32[64,128]{1,0:T(8,128)S(1)}, f32[64,128]{1,0:T(8,128)S(1)}, u32[]{:S(2)}, u32[]{:S(2)}) collective-permute-start(f32[64,128]{1,0:T(8,128)S(1)} %get-tuple-element.91), channel_id=1, source_target_pairs={{0,28},{4,0},{8,4},{12,8},{16,12},{20,16},{24,20},{28,24},{1,29},{... | collective-permute-start | bytes 98312 | tf_op jit(solution)/shard_map/ppermute | solution.py:450
  72.8 12.9 %outer.3 = (f32[128,8,128]{2,1,0:T(8,128)}, f32[128,8,128]{2,1,0:T(8,128)}) custom-call(s32[2]{0:T(128)} %get-tuple-element.44.count_ref, s32[1184]{0:T(1024)} %get-tuple-element.45.list_ref, f32[128,8,128]{2,1,0:T(8,128)} %bitcast.102, f32[8,8,128]{2,1,0:T(8,128)} %copy-done.11, f32[8,8,128]{2,1,0:T(8,128)} %copy-done.10, f32[18,8,128]{2,1,0:T(8,128)} %copy-done.18, ...), custom_call_target="tpu_custom_call" | custom-call | flops 1000000000 | bytes 4000000 | tf_op jit(solution)/shard_map/outer/pallas_call | solution.py:511
  88.8 9.5 %ocean.1 = f32[4,48,32,128]{3,2,1,0:T(8,128)} custom-call(s32[1]{0:T(128)} %bitcast.21.flags_ref, f32[4,48,32,128]{3,2,1,0:T(8,128)} %after_ref.1, f32[4,48,32,128]{3,2,1,0:T(8,128)} %after_ref.1, f32[4,48,32,128]{3,2,1,0:T(8,128)} %after_ref.1, f32[48,32,128]{2,1,0:T(8,128)} %mix_ref.1, f32[64,128]{1,0:T(8,128)} %copy-done.5, f32[64,128]{1,0:T(8,128)} %copy-done.6, ...), custom_call_target="tpu_custom_call" | custom-call | flops 100000000 | bytes 7000000 | tf_op jit(solution)/shard_map/ocean/pallas_call | solution.py:565
  101.2 7.3 %all-to-all-start.1 = ((f32[32,1,272]{2,1,0:T(1,128)}), f32[32,1,272]{2,1,0:T(1,128)S(1)}, u32[]{:S(2)}, u32[]{:S(2)}) async-start(f32[32,1,272]{2,1,0:T(1,128)} %all_to_all.16), calls=%async_computation.1 | async-start | bytes 98304 | tf_op jit(solution)/shard_map/all_to_all | solution.py:616
  108.6 3.7 %collective-permute-start.10 = (f32[18,8,128]{2,1,0:T(8,128)S(1)}, f32[18,8,128]{2,1,0:T(8,128)S(1)}, u32[]{:S(2)}, u32[]{:S(2)}) collective-permute-start(f32[18,8,128]{2,1,0:T(8,128)S(1)} %pad_maximum_fusion.3), channel_id=1, source_target_pairs={{0,1},{1,2},{2,3},{4,5},{5,6},{6,7},{8,9},{9,10},{10,11},{12,13},{... | collective-permute-start | bytes 221192 | tf_op jit(solution)/shard_map/ppermute | solution.py:411
  112.3 1.3 collective-permute-start.11
  113.6 29.9 %inner.4.inner_ref = f32[129,16,128]{2,1,0:T(8,128)} custom-call(s32[2]{0:T(128)} %get-tuple-element.44.count_ref, s32[1184]{0:T(1024)} %get-tuple-element.49.list_ref, f32[128,8,128]{2,1,0:T(8,128)} %get-tuple-element.50, bf16[9,32,384]{2,1,0:T(8,128)(2,1)} %constant.140.clone.add_ref, bf16[9,32,128]{2,1,0:T(8,128)(2,1)} %constant.141.clone.scale_ref), custom_call_target="tpu_custom_call" | custom-call | flops 8000000000 | bytes 2000000 | tf_op jit(solution)/shard_map/inner/pallas_call | solution.py:499
  144.3 12.8 %outer.4 = (f32[128,8,128]{2,1,0:T(8,128)}, f32[128,8,128]{2,1,0:T(8,128)}) custom-call(s32[2]{0:T(128)} %get-tuple-element.44.count_ref, s32[1184]{0:T(1024)} %get-tuple-element.45.list_ref, f32[128,8,128]{2,1,0:T(8,128)} %get-tuple-element.50, f32[8,8,128]{2,1,0:T(8,128)} %copy-done.13, f32[8,8,128]{2,1,0:T(8,128)} %copy-done.12, ...), custom_call_target="tpu_custom_call" | custom-call | flops 1000000000 | bytes 4000000 | tf_op jit(solution)/shard_map/outer/pallas_call | solution.py:511
  158.9 1.1 collective-permute-start.13
  160.3 1.3 collective-permute-done.13.right_ref
  161.6 2.6 %collective-permute-done.12.left_ref = f32[8,8,128]{2,1,0:T(8,128)S(1)} collective-permute-done((f32[8,8,128]{2,1,0:T(8,128)S(1)}, f32[8,8,128]{2,1,0:T(8,128)S(1)}, u32[]{:S(2)}, u32[]{:S(2)}) %collective-permute-start.12) | collective-permute-done | bytes 32800 | tf_op jit(solution)/shard_map/ppermute | solution.py:406
  164.3 5.2 %collective-permute-start.14 = (f32[18,8,128]{2,1,0:T(8,128)S(1)}, f32[18,8,128]{2,1,0:T(8,128)S(1)}, u32[]{:S(2)}, u32[]{:S(2)}) collective-permute-start(f32[18,8,128]{2,1,0:T(8,128)S(1)} %pad_maximum_fusion.5), channel_id=1, source_target_pairs={{0,1},{1,2},{2,3},{4,5},{5,6},{6,7},{8,9},{9,10},{10,11},{12,13},{... | collective-permute-start | bytes 221192 | tf_op jit(solution)/shard_map/ppermute | solution.py:411
  169.4 1.3 collective-permute-start.15
  170.7 30.1 %inner.5.inner_ref = f32[129,16,128]{2,1,0:T(8,128)} custom-call(s32[2]{0:T(128)} %get-tuple-element.44.count_ref, s32[1184]{0:T(1024)} %get-tuple-element.49.list_ref, f32[128,8,128]{2,1,0:T(8,128)} %get-tuple-element.59, bf16[9,32,384]{2,1,0:T(8,128)(2,1)} %constant.140.clone.add_ref, bf16[9,32,128]{2,1,0:T(8,128)(2,1)} %constant.141.clone.scale_ref), custom_call_target="tpu_custom_call" | custom-call | flops 8000000000 | bytes 2000000 | tf_op jit(solution)/shard_map/inner/pallas_call | solution.py:499
  201.5 12.9 %outer.5 = (f32[128,8,128]{2,1,0:T(8,128)}, f32[128,8,128]{2,1,0:T(8,128)}) custom-call(s32[2]{0:T(128)} %get-tuple-element.44.count_ref, s32[1184]{0:T(1024)} %get-tuple-element.45.list_ref, f32[128,8,128]{2,1,0:T(8,128)} %get-tuple-element.59, f32[8,8,128]{2,1,0:T(8,128)} %copy-done.15, f32[8,8,128]{2,1,0:T(8,128)} %copy-done.14, ...), custom_call_target="tpu_custom_call" | custom-call | flops 1000000000 | bytes 4000000 | tf_op jit(solution)/shard_map/outer/pallas_call | solution.py:511
  214.4 1.3 multiply_reduce_fusion
  216.6 4.6 %all-to-all-start.2 = ((f32[32,1,512]{2,1,0:T(1,128)}), f32[32,1,512]{2,1,0:T(1,128)S(1)}, u32[]{:S(2)}, u32[]{:S(2)}) async-start(f32[32,1,512]{2,1,0:T(1,128)} %broadcast_in_dim.110), calls=%async_computation.2 | async-start | bytes 131072 | tf_op jit(solution)/shard_map/all_to_all | solution.py:633
  221.6 1.1 slice.200
  224.4 4.3 %all-to-all-done.2 = f32[32,1,512]{2,1,0:T(1,128)S(1)} async-done(((f32[32,1,512]{2,1,0:T(1,128)}), f32[32,1,512]{2,1,0:T(1,128)S(1)}, u32[]{:S(2)}, u32[]{:S(2)}) %all-to-all-start.2) | async-done | bytes 65568 | tf_op jit(solution)/shard_map/all_to_all | solution.py:633
  228.8 1.1 select_reduce_fusion
  231.5 1.6 fusion.1
  (146 shorter events, 20.6 us)
Async XLA Ops:
  3.4 29.7 %collective-permute-start.1 = (f32[8,8,128]{2,1,0:T(8,128)S(1)}, f32[8,8,128]{2,1,0:T(8,128)S(1)}, u32[]{:S(2)}, u32[]{:S(2)}) collective-permute-start(f32[8,8,128]{2,1,0:T(8,128)S(1)} %get-tuple-element.84), channel_id=1, source_target_pairs={{0,28},{4,0},{8,4},{12,8},{16,12},{20,16},{24,20},{28,24},{1,29},{... | collective-permute-start | bytes 98312 | tf_op jit(solution)/shard_map/ppermute | solution.py:407
  6.8 26.3 %collective-permute-start = (f32[8,8,128]{2,1,0:T(8,128)S(1)}, f32[8,8,128]{2,1,0:T(8,128)S(1)}, u32[]{:S(2)}, u32[]{:S(2)}) collective-permute-start(f32[8,8,128]{2,1,0:T(8,128)S(1)} %get-tuple-element.83), channel_id=1, source_target_pairs={{0,4},{4,8},{8,12},{12,16},{16,20},{20,24},{24,28},{28,0},{1,5},{5... | collective-permute-start | bytes 98312 | tf_op jit(solution)/shard_map/ppermute | solution.py:406
  11.4 11.9 %copy-start.1 = (f32[8,16,128]{2,1,0:T(8,128)S(1)}, f32[8,16,128]{2,1,0:T(8,128)}, u32[]{:S(2)}) copy-start(f32[8,16,128]{2,1,0:T(8,128)} %param.18) | copy-start | bytes 196612
  11.4 11.9 %copy-start.8 = (s32[1,32,8]{1,2,0:T(8,128)S(1)}, s32[1,32,8]{1,2,0:T(8,128)}, u32[]{:S(2)}) copy-start(s32[1,32,8]{1,2,0:T(8,128)} %param.24) | copy-start | bytes 3076
  11.4 12.2 %copy-start.2 = (f32[2,8,16,128]{3,2,1,0:T(8,128)S(1)}, f32[2,8,16,128]{3,2,1,0:T(8,128)}, u32[]{:S(2)}) copy-start(f32[2,8,16,128]{3,2,1,0:T(8,128)} %param.17) | copy-start | bytes 393220
  11.4 12.3 %copy-start.16 = (s32[8]{0:T(128)S(1)}, s32[8]{0:T(128)}, u32[]{:S(2)}) copy-start(s32[8]{0:T(128)} %constant.138.clone) | copy-start | bytes 100
  11.4 12.4 %copy-start.7 = (s32[8,8,16]{2,1,0:T(8,128)S(1)}, s32[8,8,16]{2,1,0:T(8,128)}, u32[]{:S(2)}) copy-start(s32[8,8,16]{2,1,0:T(8,128)} %param.20) | copy-start | bytes 12292
  11.4 13.1 %copy-start.9 = (s32[1,32,8]{1,2,0:T(8,128)S(1)}, s32[1,32,8]{1,2,0:T(8,128)}, u32[]{:S(2)}) copy-start(s32[1,32,8]{1,2,0:T(8,128)} %param.21) | copy-start | bytes 3076
  12.3 73.3 %collective-permute-start.4 = (f32[64,128]{1,0:T(8,128)S(1)}, f32[64,128]{1,0:T(8,128)S(1)}, u32[]{:S(2)}, u32[]{:S(2)}) collective-permute-start(f32[64,128]{1,0:T(8,128)S(1)} %get-tuple-element.92), channel_id=1, source_target_pairs={{0,4},{4,8},{8,12},{12,16},{16,20},{20,24},{24,28},{28,0},{1,5},{5... | collective-permute-start | bytes 98312 | tf_op jit(solution)/shard_map/ppermute | solution.py:449
  12.3 73.4 %collective-permute-start.6 = (f32[192,128]{1,0:T(8,128)}, f32[192,128]{1,0:T(8,128)S(1)}, u32[]{:S(2)}, u32[]{:S(2)}) collective-permute-start(f32[192,128]{1,0:T(8,128)} %get-tuple-element.52), channel_id=1, source_target_pairs={{0,1},{1,2},{2,3},{4,5},{5,6},{6,7},{8,9},{9,10},{10,11},{12,13},{... | collective-permute-start | bytes 294920 | tf_op jit(solution)/shard_map/ppermute | solution.py:451
  15.8 69.9 %collective-permute-start.7 = (f32[192,128]{1,0:T(8,128)}, f32[192,128]{1,0:T(8,128)S(1)}, u32[]{:S(2)}, u32[]{:S(2)}) collective-permute-start(f32[192,128]{1,0:T(8,128)} %get-tuple-element.53), channel_id=1, source_target_pairs={{1,0},{2,1},{3,2},{5,4},{6,5},{7,6},{9,8},{10,9},{11,10},{13,12},{... | collective-permute-start | bytes 294920 | tf_op jit(solution)/shard_map/ppermute | solution.py:452
  19.0 66.8 %all-to-all-start = ((f32[8,192,128]{2,1,0:T(8,128)}), f32[8,192,128]{2,1,0:T(8,128)S(1)}, u32[]{:S(2)}, u32[]{:S(2)}) async-start(f32[8,192,128]{2,1,0:T(8,128)} %broadcast_in_dim.103), calls=%async_computation | async-start | bytes 1572864 | tf_op jit(solution)/shard_map/all_to_all | solution.py:454
  33.1 36.6 %copy-start.10 = (f32[8,8,128]{2,1,0:T(8,128)}, f32[8,8,128]{2,1,0:T(8,128)S(1)}, u32[]{:S(2)}) copy-start(f32[8,8,128]{2,1,0:T(8,128)S(1)} %collective-permute-done.1.right_ref) | copy-start | bytes 98308
  33.1 36.6 %copy-start.11 = (f32[8,8,128]{2,1,0:T(8,128)}, f32[8,8,128]{2,1,0:T(8,128)S(1)}, u32[]{:S(2)}) copy-start(f32[8,8,128]{2,1,0:T(8,128)S(1)} %collective-permute-done.left_ref) | copy-start | bytes 98308
  34.0 35.7 %collective-permute-start.2 = (f32[18,8,128]{2,1,0:T(8,128)S(1)}, f32[18,8,128]{2,1,0:T(8,128)S(1)}, u32[]{:S(2)}, u32[]{:S(2)}) collective-permute-start(f32[18,8,128]{2,1,0:T(8,128)S(1)} %get-tuple-element.47), channel_id=1, source_target_pairs={{0,1},{1,2},{2,3},{4,5},{5,6},{6,7},{8,9},{9,10},{10,11},{12,13},{... | collective-permute-start | bytes 221192 | tf_op jit(solution)/shard_map/ppermute | solution.py:411
  38.6 33.6 %collective-permute-start.3 = (f32[18,8,128]{2,1,0:T(8,128)S(1)}, f32[18,8,128]{2,1,0:T(8,128)S(1)}, u32[]{:S(2)}, u32[]{:S(2)}) collective-permute-start(f32[18,8,128]{2,1,0:T(8,128)S(1)} %get-tuple-element.48), channel_id=1, source_target_pairs={{1,0},{2,1},{3,2},{5,4},{6,5},{7,6},{9,8},{10,9},{11,10},{13,12},{... | collective-permute-start | bytes 221192 | tf_op jit(solution)/shard_map/ppermute | solution.py:412
  69.8 15.9 %collective-permute-start.5 = (f32[64,128]{1,0:T(8,128)S(1)}, f32[64,128]{1,0:T(8,128)S(1)}, u32[]{:S(2)}, u32[]{:S(2)}) collective-permute-start(f32[64,128]{1,0:T(8,128)S(1)} %get-tuple-element.91), channel_id=1, source_target_pairs={{0,28},{4,0},{8,4},{12,8},{16,12},{20,16},{24,20},{28,24},{1,29},{... | collective-permute-start | bytes 98312 | tf_op jit(solution)/shard_map/ppermute | solution.py:450
  85.7 3.1 %copy-start.5 = (f32[64,128]{1,0:T(8,128)}, f32[64,128]{1,0:T(8,128)S(1)}, u32[]{:S(2)}) copy-start(f32[64,128]{1,0:T(8,128)S(1)} %collective-permute-done.4.west_ref) | copy-start | bytes 98308
  87.5 21.0 %collective-permute-start.9 = (f32[8,8,128]{2,1,0:T(8,128)S(1)}, f32[8,8,128]{2,1,0:T(8,128)S(1)}, u32[]{:S(2)}, u32[]{:S(2)}) collective-permute-start(f32[8,8,128]{2,1,0:T(8,128)S(1)} %get-tuple-element.80), channel_id=1, source_target_pairs={{0,28},{4,0},{8,4},{12,8},{16,12},{20,16},{24,20},{28,24},{1,29},{... | collective-permute-start | bytes 98312 | tf_op jit(solution)/shard_map/ppermute | solution.py:407
  87.6 21.0 %collective-permute-start.8 = (f32[8,8,128]{2,1,0:T(8,128)S(1)}, f32[8,8,128]{2,1,0:T(8,128)S(1)}, u32[]{:S(2)}, u32[]{:S(2)}) collective-permute-start(f32[8,8,128]{2,1,0:T(8,128)S(1)} %get-tuple-element.79), channel_id=1, source_target_pairs={{0,4},{4,8},{8,12},{12,16},{16,20},{20,24},{24,28},{28,0},{1,5},{5... | collective-permute-start | bytes 98312 | tf_op jit(solution)/shard_map/ppermute | solution.py:406
  101.2 42.3 %all-to-all-start.1 = ((f32[32,1,272]{2,1,0:T(1,128)}), f32[32,1,272]{2,1,0:T(1,128)S(1)}, u32[]{:S(2)}, u32[]{:S(2)}) async-start(f32[32,1,272]{2,1,0:T(1,128)} %all_to_all.16), calls=%async_computation.1 | async-start | bytes 98304 | tf_op jit(solution)/shard_map/all_to_all | solution.py:616
  108.5 35.0 %copy-start.12 = (f32[8,8,128]{2,1,0:T(8,128)}, f32[8,8,128]{2,1,0:T(8,128)S(1)}, u32[]{:S(2)}) copy-start(f32[8,8,128]{2,1,0:T(8,128)S(1)} %collective-permute-done.9.right_ref) | copy-start | bytes 98308
  108.6 35.0 %copy-start.13 = (f32[8,8,128]{2,1,0:T(8,128)}, f32[8,8,128]{2,1,0:T(8,128)S(1)}, u32[]{:S(2)}) copy-start(f32[8,8,128]{2,1,0:T(8,128)S(1)} %collective-permute-done.8.left_ref) | copy-start | bytes 98308
  108.6 35.0 %collective-permute-start.10 = (f32[18,8,128]{2,1,0:T(8,128)S(1)}, f32[18,8,128]{2,1,0:T(8,128)S(1)}, u32[]{:S(2)}, u32[]{:S(2)}) collective-permute-start(f32[18,8,128]{2,1,0:T(8,128)S(1)} %pad_maximum_fusion.3), channel_id=1, source_target_pairs={{0,1},{1,2},{2,3},{4,5},{5,6},{6,7},{8,9},{9,10},{10,11},{12,13},{... | collective-permute-start | bytes 221192 | tf_op jit(solution)/shard_map/ppermute | solution.py:411
  112.3 31.4 %collective-permute-start.11 = (f32[18,8,128]{2,1,0:T(8,128)S(1)}, f32[18,8,128]{2,1,0:T(8,128)S(1)}, u32[]{:S(2)}, u32[]{:S(2)}) collective-permute-start(f32[18,8,128]{2,1,0:T(8,128)S(1)} %pad_maximum_fusion.2), channel_id=1, source_target_pairs={{1,0},{2,1},{3,2},{5,4},{6,5},{7,6},{9,8},{10,9},{11,10},{13,12},{... | collective-permute-start | bytes 221192 | tf_op jit(solution)/shard_map/ppermute | solution.py:412
  158.9 2.7 %collective-permute-start.13 = (f32[8,8,128]{2,1,0:T(8,128)S(1)}, f32[8,8,128]{2,1,0:T(8,128)S(1)}, u32[]{:S(2)}, u32[]{:S(2)}) collective-permute-start(f32[8,8,128]{2,1,0:T(8,128)S(1)} %get-tuple-element.76), channel_id=1, source_target_pairs={{0,28},{4,0},{8,4},{12,8},{16,12},{20,16},{24,20},{28,24},{1,29},{... | collective-permute-start | bytes 98312 | tf_op jit(solution)/shard_map/ppermute | solution.py:407
  160.0 4.2 %collective-permute-start.12 = (f32[8,8,128]{2,1,0:T(8,128)S(1)}, f32[8,8,128]{2,1,0:T(8,128)S(1)}, u32[]{:S(2)}, u32[]{:S(2)}) collective-permute-start(f32[8,8,128]{2,1,0:T(8,128)S(1)} %get-tuple-element.75), channel_id=1, source_target_pairs={{0,4},{4,8},{8,12},{12,16},{16,20},{20,24},{24,28},{28,0},{1,5},{5... | collective-permute-start | bytes 98312 | tf_op jit(solution)/shard_map/ppermute | solution.py:406
  161.6 39.2 %copy-start.14 = (f32[8,8,128]{2,1,0:T(8,128)}, f32[8,8,128]{2,1,0:T(8,128)S(1)}, u32[]{:S(2)}) copy-start(f32[8,8,128]{2,1,0:T(8,128)S(1)} %collective-permute-done.13.right_ref) | copy-start | bytes 98308
  164.2 36.6 %copy-start.15 = (f32[8,8,128]{2,1,0:T(8,128)}, f32[8,8,128]{2,1,0:T(8,128)S(1)}, u32[]{:S(2)}) copy-start(f32[8,8,128]{2,1,0:T(8,128)S(1)} %collective-permute-done.12.left_ref) | copy-start | bytes 98308
  164.3 36.6 %collective-permute-start.14 = (f32[18,8,128]{2,1,0:T(8,128)S(1)}, f32[18,8,128]{2,1,0:T(8,128)S(1)}, u32[]{:S(2)}, u32[]{:S(2)}) collective-permute-start(f32[18,8,128]{2,1,0:T(8,128)S(1)} %pad_maximum_fusion.5), channel_id=1, source_target_pairs={{0,1},{1,2},{2,3},{4,5},{5,6},{6,7},{8,9},{9,10},{10,11},{12,13},{... | collective-permute-start | bytes 221192 | tf_op jit(solution)/shard_map/ppermute | solution.py:411
  169.4 31.4 %collective-permute-start.15 = (f32[18,8,128]{2,1,0:T(8,128)S(1)}, f32[18,8,128]{2,1,0:T(8,128)S(1)}, u32[]{:S(2)}, u32[]{:S(2)}) collective-permute-start(f32[18,8,128]{2,1,0:T(8,128)S(1)} %pad_maximum_fusion.4), channel_id=1, source_target_pairs={{1,0},{2,1},{3,2},{5,4},{6,5},{7,6},{9,8},{10,9},{11,10},{13,12},{... | collective-permute-start | bytes 221192 | tf_op jit(solution)/shard_map/ppermute | solution.py:412
  216.6 12.1 %all-to-all-start.2 = ((f32[32,1,512]{2,1,0:T(1,128)}), f32[32,1,512]{2,1,0:T(1,128)S(1)}, u32[]{:S(2)}, u32[]{:S(2)}) async-start(f32[32,1,512]{2,1,0:T(1,128)} %broadcast_in_dim.110), calls=%async_computation.2 | async-start | bytes 131072 | tf_op jit(solution)/shard_map/all_to_all | solution.py:633
  (10 other events, 17.7 us)
